TPU v7x, 32 devices: a 4x2x2 block of a 4x4x8 slice. The times are simulated.
32 devices in a mesh: replica: 4 (over y, z), dp: 8 (over x, core).
Axes of the slice: x: 4, y: 2, z: 2, core: 2. Of those that a mesh axis runs over, the one named last changes fastest.
The devices are a block of a 4x4x8 slice.
Arguments:
- x: bfloat16 [2048, 2048], P(('replica', 'dp')), parts along dimension 0
- lengths: int32 [2048], P(('replica', 'dp')), parts along dimension 0
- cache: bfloat16 [2, 2048, 128, 576], P(None, ('replica', 'dp')), parts along dimension 1
- attn_gain: float32 [2, 2048], replicated
- ffn_gain: float32 [2, 2048], replicated
- w_query: bfloat16 [2, 2048, 9216], replicated
- w_attn_out: bfloat16 [2, 8192, 2048], replicated
- w_up: bfloat16 [2, 2048, 11264], P(None, None, 'dp')
- w_gate: bfloat16 [2, 2048, 11264], P(None, None, 'dp')
- w_down: bfloat16 [2, 11264, 2048], P(None, 'dp')
Outputs:
- output: bfloat16 [2048, 2048], P(('replica', 'dp')), parts along dimension 0
There are 4 independent parts. A program takes and returns all parts, laid end to end along the dimension named above; an argument that names none is the same for every part.
All inputs are finite; a program needn't handle non-finite values.
Results may differ from a plain program's by a relative error of at most 0.02.
Values are sent between devices in bfloat16 or wider.
A program may use at most 768 MiB of HBM per device.

v0:
```python
import jax
import jax.numpy as jnp
from jax import lax
from jax.sharding import PartitionSpec as P

NORM_EPS = 1e-6


def rms_norm(rows, gain):
    rows_f = rows.astype(jnp.float32)
    mean_sq = jnp.mean(rows_f * rows_f, axis=-1, keepdims=True)
    return (rows_f * lax.rsqrt(mean_sq + NORM_EPS) * gain).astype(jnp.bfloat16)


def local_attention(x_rows, len_rows, cache_l, gain, wq_l, wo_l):
    rows, seq_len, kv_dim = cache_l.shape
    heads = wq_l.shape[1] // kv_dim
    latent = wo_l.shape[0] // heads
    d_model = wo_l.shape[1]
    scale = (3 * (kv_dim - latent)) ** -0.5
    normed = rms_norm(x_rows, gain)
    query = jnp.dot(normed, wq_l, preferred_element_type=jnp.float32).astype(jnp.bfloat16)
    query = query.reshape(rows, heads, kv_dim)
    scores = jnp.einsum('bhc,btc->bht', query, cache_l, preferred_element_type=jnp.float32) * scale
    positions = lax.broadcasted_iota(jnp.int32, (1, 1, seq_len), 2)
    scores = jnp.where(positions < len_rows[:, None, None], scores, -jnp.inf)
    attn_probs = jax.nn.softmax(scores, axis=-1).astype(jnp.bfloat16)
    mixed = jnp.einsum('bht,btc->bhc', attn_probs, cache_l, preferred_element_type=jnp.float32)
    mixed = mixed[:, :, :latent].astype(jnp.bfloat16)
    attn_out = jnp.einsum('bhc,hcd->bd', mixed, wo_l.reshape(heads, latent, d_model), preferred_element_type=jnp.float32)
    return (x_rows.astype(jnp.float32) + attn_out).astype(jnp.bfloat16)


def solution(mesh):
    row_axes = ('replica', 'dp')

    def local_step(x_rows, len_rows, cache, attn_gain, ffn_gain, w_query, w_attn_out, w_up, w_gate, w_down):
        for layer_idx in range(cache.shape[0]):
            x_rows = local_attention(x_rows, len_rows, cache[layer_idx], attn_gain[layer_idx], w_query[layer_idx], w_attn_out[layer_idx])
            normed = rms_norm(x_rows, ffn_gain[layer_idx])
            gathered = lax.all_gather(normed, 'dp', axis=0, tiled=True)
            gate_pre = jnp.dot(gathered, w_gate[layer_idx], preferred_element_type=jnp.float32)
            up_pre = jnp.dot(gathered, w_up[layer_idx], preferred_element_type=jnp.float32)
            hidden = (jax.nn.silu(gate_pre) * up_pre).astype(jnp.bfloat16)
            partial_out = jnp.dot(hidden, w_down[layer_idx], preferred_element_type=jnp.float32)
            ffn_rows = lax.psum_scatter(partial_out, 'dp', scatter_dimension=0, tiled=True)
            x_rows = (x_rows.astype(jnp.float32) + ffn_rows).astype(jnp.bfloat16)
        return x_rows

    return jax.shard_map(
        local_step,
        mesh=mesh,
        in_specs=(P(row_axes, None), P(row_axes), P(None, row_axes, None, None), P(), P(), P(), P(),
                  P(None, None, 'dp'), P(None, None, 'dp'), P(None, 'dp', None)),
        out_specs=P(row_axes, None),
        check_vma=False,
    )
```

profile of v0, /device:TPU:81, one launch (start us, length us, event | category | flops | bytes accessed | tf_op | source)
XLA Modules:
  0.0 308.7 jit_solution(11630899217924352804)
XLA Ops:
  6.6 0.8 fusion.102
  7.4 1.1 fusion.82
  8.5 15.3 %fusion.8 = bf16[64,9216]{1,0:T(8,128)(2,1)S(1)} fusion(bf16[2,2048,9216]{2,1,0:T(8,128)(2,1)} %param.15, bf16[64,2048]{1,0:T(8,128)(2,1)} %param.10, f32[2048]{0:T(1024)S(1)} %bitcast.97, f32[64]{0:T(128)S(1)} %add_rsqrt_fusion.3), kind=kOutput, calls=%fused_computation.8 | convolution fusion | flops 2417033216 | bytes 39198976 | tf_op jit(solution)/shard_map/dot_general | solution.py:22
  23.8 1.1 reshape.63
  25.0 4.6 %fusion.79 = f32[64,16,128]{2,1,0:T(8,128)S(1)} fusion(bf16[64,16,576]{2,1,0:T(8,128)(2,1)S(1)} %reshape.63, bf16[2,64,128,576]{2,3,1,0:T(8,128)(2,1)} %param.12, pred[64,128]{1,0:T(8,128)(4,1)S(1)} %iota_compare_fusion), kind=kOutput, calls=%fused_computation.61 | convolution fusion | flops 151257088 | bytes 11149312 | tf_op jit(solution)/shard_map/bhc,btc->bht/dot_general | solution.py:24
  29.6 0.3 fusion.103
  29.9 6.6 %fusion.18 = bf16[64,16,576]{2,1,0:T(8,128)(2,1)S(1)} fusion(bf16[2,64,128,576]{2,3,1,0:T(8,128)(2,1)} %param.12, f32[64,16]{1,0:T(8,128)S(1)} %fusion.103, f32[64,16,128]{2,1,0:T(8,128)S(1)} %fusion.79), kind=kOutput, calls=%fused_computation.14 | convolution fusion | flops 151389312 | bytes 11698176 | tf_op jit(solution)/shard_map/bht,btc->bhc/dot_general | solution.py:28
  36.5 0.1 slice.74
  36.7 44.7 %fusion.100 = (bf16[1,8192,2048]{2,1,0:T(8,128)(2,1)}, bf16[1,8192,2048]{2,1,0:T(8,128)(2,1)}) fusion(bf16[2,8192,2048]{2,1,0:T(8,128)(2,1)} %param.16), kind=kLoop, calls=%fused_computation.95 | loop fusion | bytes 134217728 | tf_op jit(solution)/shard_map/slice | solution.py:39
  81.4 14.3 %multiply_reduce_fusion.1 = (f32[64]{0:T(128)S(1)}, f32[64,2048]{1,0:T(8,128)S(1)}) fusion(bf16[16,512,2048]{2,1,0:T(8,128)(2,1)} %bitcast.93, bf16[64,16,512]{2,1,0:T(8,128)(2,1)S(1)} %slice.74, bf16[64,2048]{1,0:T(8,128)(2,1)S(1)} %copy-done), kind=kOutput, calls=%fused_computation.78 | convolution fusion | flops 2148270080 | bytes 35389696 | tf_op jit(solution)/shard_map/bhc,hcd->bd/dot_general | solution.py:30
  95.7 0.8 multiply_convert_fusion.1
  96.6 0.2 reduce-scatter.3.cloned.1.call-start
  96.9 26.4 %all-gather.3.cloned.1.call-done = bf16[512,2048]{1,0:T(8,128)(2,1)} async-done(((bf16[64,2048]{1,0:T(8,128)(2,1)}), bf16[512,2048]{1,0:T(8,128)(2,1)}) %all-gather.3.cloned.1.call-update) | async-done | bytes 2097168 | tf_op jit(solution)/shard_map/all_gather | solution.py:41
  123.3 8.4 %fusion.36 = f32[512,1408]{1,0:T(8,128)} fusion(bf16[512,2048]{1,0:T(8,128)(2,1)} %all-gather.3.cloned.1.call-done, bf16[2,2048,1408]{2,1,0:T(8,128)(2,1)} %param.18), kind=kOutput, calls=%fused_computation.32 | convolution fusion | flops 2952790016 | bytes 10747904 | tf_op jit(solution)/shard_map/dot_general | solution.py:42
  131.7 13.9 %fusion.32 = f32[512,2048]{1,0:T(8,128)} fusion(bf16[2,1408,2048]{2,1,0:T(8,128)(2,1)} %param.19, bf16[512,2048]{1,0:T(8,128)(2,1)S(1)} %copy-done.3, bf16[2,2048,1408]{2,1,0:T(8,128)(2,1)} %param.17, f32[512,1408]{1,0:T(8,128)} %fusion.36), kind=kOutput, calls=%fused_computation.28 | convolution fusion | flops 5909905408 | bytes 20709376 | tf_op jit(solution)/shard_map/dot_general | solution.py:45
  145.7 0.3 all-gather.5.cloned.1.call-start
  145.9 32.0 %reduce-scatter.3.cloned.1.call-done = f32[64,2048]{1,0:T(8,128)} async-done(((f32[512,2048]{1,0:T(8,128)}), f32[64,2048]{1,0:T(8,128)}) %reduce-scatter.3.cloned.1.call-update) | async-done | bytes 524304 | tf_op jit(solution)/shard_map/reduce_scatter | solution.py:46
  178.0 1.2 fusion.85
  179.2 14.1 %fusion.11 = bf16[64,9216]{1,0:T(8,128)(2,1)S(1)} fusion(bf16[2,2048,9216]{2,1,0:T(8,128)(2,1)} %param.15, bf16[64,2048]{1,0:T(8,128)(2,1)S(1)} %get-tuple-element.6, f32[2048]{0:T(1024)S(1)} %bitcast.96, f32[64]{0:T(128)S(1)} %add_rsqrt_fusion.1), kind=kOutput, calls=%fused_computation.9 | convolution fusion | flops 2417033216 | bytes 39198976 | tf_op jit(solution)/shard_map/dot_general | solution.py:22
  193.3 1.1 reshape.64
  194.4 4.6 %fusion.76 = f32[64,16,128]{2,1,0:T(8,128)S(1)} fusion(bf16[64,16,576]{2,1,0:T(8,128)(2,1)S(1)} %reshape.64, bf16[2,64,128,576]{2,3,1,0:T(8,128)(2,1)} %param.12, pred[64,128]{1,0:T(8,128)(4,1)S(1)} %iota_compare_fusion), kind=kOutput, calls=%fused_computation.60 | convolution fusion | flops 151257088 | bytes 11149312 | tf_op jit(solution)/shard_map/bhc,btc->bht/dot_general | solution.py:24
  199.0 0.3 fusion.104
  199.3 6.6 %fusion.14 = bf16[64,16,576]{2,1,0:T(8,128)(2,1)S(1)} fusion(bf16[2,64,128,576]{2,3,1,0:T(8,128)(2,1)} %param.12, f32[64,16]{1,0:T(8,128)S(1)} %fusion.104, f32[64,16,128]{2,1,0:T(8,128)S(1)} %fusion.76), kind=kOutput, calls=%fused_computation.10 | convolution fusion | flops 151389312 | bytes 11698176 | tf_op jit(solution)/shard_map/bht,btc->bhc/dot_general | solution.py:28
  205.9 0.1 slice.75
  206.1 14.5 %multiply_reduce_fusion = (f32[64]{0:T(128)S(1)}, f32[64,2048]{1,0:T(8,128)S(1)}) fusion(bf16[16,512,2048]{2,1,0:T(8,128)(2,1)} %bitcast.92, bf16[64,16,512]{2,1,0:T(8,128)(2,1)S(1)} %slice.75, bf16[64,2048]{1,0:T(8,128)(2,1)S(1)} %get-tuple-element.6), kind=kOutput, calls=%fused_computation.74 | convolution fusion | flops 2148270080 | bytes 35389696 | tf_op jit(solution)/shard_map/bhc,hcd->bd/dot_general | solution.py:30
  220.5 0.8 multiply_convert_fusion
  221.4 0.3 reduce-scatter.5.cloned.1.call-start
  221.8 23.9 %all-gather.5.cloned.1.call-done = bf16[512,2048]{1,0:T(8,128)(2,1)} async-done(((bf16[64,2048]{1,0:T(8,128)(2,1)}), bf16[512,2048]{1,0:T(8,128)(2,1)}) %all-gather.5.cloned.1.call-update) | async-done | bytes 2097168 | tf_op jit(solution)/shard_map/all_gather | solution.py:41
  245.7 8.4 %fusion.30 = f32[512,1408]{1,0:T(8,128)} fusion(bf16[512,2048]{1,0:T(8,128)(2,1)} %all-gather.5.cloned.1.call-done, bf16[2,2048,1408]{2,1,0:T(8,128)(2,1)} %param.18), kind=kOutput, calls=%fused_computation.26 | convolution fusion | flops 2952790016 | bytes 10747904 | tf_op jit(solution)/shard_map/dot_general | solution.py:42
  254.1 13.8 %fusion.26 = f32[512,2048]{1,0:T(8,128)} fusion(bf16[2,1408,2048]{2,1,0:T(8,128)(2,1)} %param.19, bf16[512,2048]{1,0:T(8,128)(2,1)S(1)} %copy-done.4, bf16[2,2048,1408]{2,1,0:T(8,128)(2,1)} %param.17, f32[512,1408]{1,0:T(8,128)} %fusion.30), kind=kOutput, calls=%fused_computation.22 | convolution fusion | flops 5909905408 | bytes 20709376 | tf_op jit(solution)/shard_map/dot_general | solution.py:45
  268.0 32.3 %reduce-scatter.5.cloned.1.call-done = f32[64,2048]{1,0:T(8,128)} async-done(((f32[512,2048]{1,0:T(8,128)}), f32[64,2048]{1,0:T(8,128)}) %reduce-scatter.5.cloned.1.call-update) | async-done | bytes 524304 | tf_op jit(solution)/shard_map/reduce_scatter | solution.py:46
  300.3 1.8 add_convert_fusion
  (21 shorter events, 0.4 us)
Async XLA Ops:
  6.5 116.7 %all-gather.3.cloned.1.call-start = ((), (), s32[]{:S(2)}) async-start(), calls=%async_computation.2 | async-start | bytes 2359296 | tf_op jit(solution)/shard_map/all_gather | solution.py:41
  8.5 16.4 %copy-start.2 = (s32[64]{0:T(128)S(1)}, s32[64]{0:T(128)}, u32[]{:S(2)}) copy-start(s32[64]{0:T(128)} %param.11) | copy-start | bytes 772
  36.6 44.7 %copy-start = (bf16[64,2048]{1,0:T(8,128)(2,1)S(1)}, bf16[64,2048]{1,0:T(8,128)(2,1)}, u32[]{:S(2)}) copy-start(bf16[64,2048]{1,0:T(8,128)(2,1)} %param.10) | copy-start | bytes 786436
  81.4 14.4 %copy-start.1 = (f32[2,2048]{1,0:T(2,128)S(1)}, f32[2,2048]{1,0:T(2,128)}, u32[]{:S(2)}) copy-start(f32[2,2048]{1,0:T(2,128)} %param.14) | copy-start | bytes 49156
  96.6 81.4 %reduce-scatter.3.cloned.1.call-start = ((), (), s32[]{:S(2)}) async-start(), calls=%async_computation.3 | async-start | bytes 4718592 | tf_op jit(solution)/shard_map/reduce_scatter | solution.py:46
  123.3 8.4 %copy-start.3 = (bf16[512,2048]{1,0:T(8,128)(2,1)S(1)}, bf16[512,2048]{1,0:T(8,128)(2,1)}, u32[]{:S(2)}) copy-start(bf16[512,2048]{1,0:T(8,128)(2,1)} %all-gather.3.cloned.1.call-done) | copy-start | bytes 6291460
  145.7 100.1 %all-gather.5.cloned.1.call-start = ((), (), s32[]{:S(2)}) async-start(), calls=%async_computation.4 | async-start | bytes 2359296 | tf_op jit(solution)/shard_map/all_gather | solution.py:41
  221.4 78.9 %reduce-scatter.5.cloned.1.call-start = ((), (), s32[]{:S(2)}) async-start(), calls=%async_computation.5 | async-start | bytes 4718592 | tf_op jit(solution)/shard_map/reduce_scatter | solution.py:46
  245.7 8.4 %copy-start.4 = (bf16[512,2048]{1,0:T(8,128)(2,1)S(1)}, bf16[512,2048]{1,0:T(8,128)(2,1)}, u32[]{:S(2)}) copy-start(bf16[512,2048]{1,0:T(8,128)(2,1)} %all-gather.5.cloned.1.call-done) | copy-start | bytes 6291460
Sparse Core Ops, SparseCore 0:
  96.7 26.4 all-gather.2
  145.8 32.1 reduce-scatter.2
  221.5 24.1 all-gather.4
  268.1 32.1 reduce-scatter.4
where the time goes:
time: 311 us; the launch traced here: 309 us
  matrix products  125 us (40%)
  waiting for transfers between devices  115 us (37%)
  local copies, waits for them, and re-layouts  48.1 us (15%)
  between operations  13.3 us (4%)
  other arithmetic  6.53 us (2%)
    reduce_scatter x2, waiting for transfers between devices, local_step(): lax.psum_scatter(partial_out, 'dp', scatter_dimension=0, tiled=True)  64.4 us
    all_gather x2, waiting for transfers between devices, local_step(): gathered = lax.all_gather(normed, 'dp', axis=0, tiled=True)  50.4 us
    slice x1, local copies, waits for them, and re-layouts, local_step(): w_attn_out[layer_idx]  44.7 us
    dot_general x2, matrix products, local_attention(): jnp.dot(normed, wq_l, preferred_element_type=jnp.float32)  29.3 us
    dot_general x2, matrix products, local_attention(): jnp.einsum('bhc,hcd->bd', mixed, wo_l.reshape(heads, latent, d_model), pr...  28.8 us
    dot_general x2, matrix products, local_step(): jnp.dot(hidden, w_down[layer_idx], preferred_element_type=jnp.float32)  27.7 us
    dot_general x2, matrix products, local_step(): jnp.dot(gathered, w_gate[layer_idx], preferred_element_type=jnp.float32)  16.8 us
    dot_general x2, matrix products, local_attention(): jnp.einsum('bht,btc->bhc', attn_probs, cache_l, preferred_element_type=jn...  13.1 us
  transfers between devices with their start and end apart: 4, of which 4 were waited for; matrix products, arithmetic and copies ran while one was open for 0% of the time, Pallas kernels for 0%

commit v1 on v0

v1 whole, which is shorter than its diff:
```python
import functools

import jax
import jax.numpy as jnp
from jax import lax
from jax.experimental import pallas as pl
from jax.experimental.pallas import tpu as pltpu
from jax.sharding import PartitionSpec as P

NORM_EPS = 1e-6
BF = jnp.bfloat16
F32 = jnp.float32
GRP = 16
OBLK = 256


def kernel(dims, x_hbm, lens, cache_hbm, ga_ref, gf_ref, wq_hbm, wo_hbm, wu_hbm, wg_hbm, wd_hbm, out_hbm,
           r1, r2, r3, xfull, hbuf, q3, qs, sbuf, pbuf, o3, oall, xg, sown, prd, pst, hid, rb,
           sem_w, sem_c, sem_o, sem_f, sem_x, xi_s, xi_r, q_s, q_r, o_s, o_r, ag_s, ag_r, pd_s, pd_r, rs_s, rs_r,
           xx_s, xx_r):
    layers, rows, seq, kv, heads, latent, d, ff, chips = dims
    half = d // 2
    qh = heads * kv // 2
    qblk = qh // 4
    scale = (3 * (kv - latent)) ** -0.5
    n_grp = rows // GRP
    n_ob = half // OBLK
    n_lt = pl.cdiv(kv, 128)

    me = lax.axis_index('dp')
    c = lax.rem(me, 2)
    chip = me // 2
    partner = me + 1 - 2 * c
    right = lax.rem(chip + 1, chips) * 2 + c
    left = lax.rem(chip + chips - 1, chips) * 2 + c
    ch_r = lax.rem(chip + 1, chips)
    ch_l = lax.rem(chip + chips - 1, chips)
    ch_o = lax.rem(chip + 2, chips)

    def rc(src, dst, ss, rs, dev):
        return pltpu.make_async_remote_copy(src_ref=src, dst_ref=dst, send_sem=ss, recv_sem=rs,
                                            device_id={'dp': dev}, device_id_type=pl.DeviceIdType.MESH)

    def wq_copy(l, i):
        cols = pl.ds(pl.multiple_of(c * qh + i * qblk, 128), qblk)
        return pltpu.make_async_copy(wq_hbm.at[l, :, cols], r1.at[:, pl.ds(i * qblk, qblk)], sem_w.at[i])

    def c_copy(l, g):
        rs = pl.ds(pl.multiple_of(g * GRP, GRP), GRP)
        return pltpu.make_async_copy(cache_hbm.at[l, rs], r3.at[rs], sem_c.at[g])

    def wo_copy(l, nb):
        cols = pl.ds(pl.multiple_of(c * half + nb * OBLK, 128), OBLK)
        return pltpu.make_async_copy(wo_hbm.at[l, :, cols], r2.at[nb], sem_o.at[nb])

    def ffn_copies(l):
        lo = pl.ds(pl.multiple_of((1 - c) * half, 128), half)
        hi = pl.ds(pl.multiple_of(c * half, 128), half)
        return (
            pltpu.make_async_copy(wg_hbm.at[l], r1.at[:, pl.ds(0, ff)], sem_f.at[0]),
            pltpu.make_async_copy(wu_hbm.at[l], r1.at[:, pl.ds(ff, ff)], sem_f.at[1]),
            pltpu.make_async_copy(wd_hbm.at[l, :, lo], r1.at[pl.ds(0, ff), pl.ds(2 * ff, half)], sem_f.at[2]),
            pltpu.make_async_copy(wd_hbm.at[l, :, hi], r1.at[pl.ds(0, ff), pl.ds(2 * ff + half, half)], sem_f.at[3]),
        )

    x_in = [pltpu.make_async_copy(x_hbm.at[:, pl.ds(k * half, half)], xfull.at[k, pl.ds(0, rows)], sem_x.at[k])
            for k in range(2)]
    for cp in x_in:
        cp.start()
    for i in range(4):
        wq_copy(0, i).start()

    barrier = pltpu.get_barrier_semaphore()
    for dev in (partner, left, right):
        pl.semaphore_signal(barrier, inc=1, device_id={'dp': dev}, device_id_type=pl.DeviceIdType.MESH)
    pl.semaphore_wait(barrier, 3)

    x_out = [rc(x_hbm.at[:, pl.ds(k * half, half)], xfull.at[k, pl.ds(rows, rows)], xi_s.at[k], xi_r.at[k], partner)
             for k in range(2)]
    for cp in x_out:
        cp.start()
    for cp in x_in:
        cp.wait()
    for cp in x_out:
        cp.wait()

    def norm_rows(src, gain):
        scales = []
        for r in range(2 * rows // 16):
            a = src[0, pl.ds(r * 16, 16), :].astype(F32)
            b = src[1, pl.ds(r * 16, 16), :].astype(F32)
            ms = jnp.sum(a * a + b * b, axis=-1, keepdims=True) * (1.0 / d)
            scales.append(lax.rsqrt(ms + NORM_EPS))
        for r in range(2 * rows // 16):
            for k in range(2):
                a = src[k, pl.ds(r * 16, 16), :].astype(F32)
                hbuf[pl.ds(r * 16, 16), pl.ds(k * half, half)] = (
                    a * scales[r] * gain[:, k * half:(k + 1) * half]).astype(BF)

    def layer_body(l, carry):
        norm_rows(xfull, ga_ref[pl.ds(l, 1), :])
        q_sends = []
        for i in range(4):
            wq_copy(l, i).wait()

            @pl.when(l == 0)
            def _():
                if i < 2:
                    c_copy(0, 2 * i).start()
                    c_copy(0, 2 * i + 1).start()
                else:
                    wo_copy(0, 2 * (i - 2)).start()
                    wo_copy(0, 2 * (i - 2) + 1).start()

            acc = jnp.dot(hbuf[...], r1[:, i * qblk:(i + 1) * qblk], preferred_element_type=F32)
            acc = acc.astype(BF).astype(F32)
            rolled = pltpu.roll(acc, kv, 1)
            base = pl.multiple_of((c * (heads // 2) + 2 * i) * rows, rows)
            for t in range(n_lt):
                lanes = slice(t * 128, (t + 1) * 128)
                q3[t, pl.ds(base, rows), :] = acc[:rows, lanes]
                q3[t, pl.ds(base + rows, rows), :] = rolled[:rows, lanes]
                qs[t, pl.ds(2 * i * rows, rows), :] = acc[rows:, lanes]
                qs[t, pl.ds((2 * i + 1) * rows, rows), :] = rolled[rows:, lanes]
            cp = rc(qs.at[:, pl.ds(2 * i * rows, 2 * rows)], q3.at[:, pl.ds(base, 2 * rows)], q_s.at[i], q_r.at[i],
                    partner)
            cp.start()
            q_sends.append(cp)
        for cp in ffn_copies(l):
            cp.start()
        for cp in q_sends:
            cp.wait()

        def o_copy(g):
            src = oall.at[:, pl.ds(pl.multiple_of(g * GRP, GRP), GRP)]
            dst = oall.at[:, pl.ds(pl.multiple_of(rows + g * GRP, GRP), GRP)]
            return rc(src, dst, o_s.at[g], o_r.at[g], partner)

        pos = lax.broadcasted_iota(jnp.int32, (heads, seq), 1)
        first = lax.rem(lax.broadcasted_iota(jnp.int32, (GRP * heads, seq), 0), 2 * heads) < heads

        def attn_group(g, carry):
            c_copy(l, g).wait()
            for b in range(0, GRP, 2):
                row = g * GRP + b
                qb = jnp.concatenate(
                    [jnp.concatenate([q3[t, pl.ds(row + k, heads, stride=rows), :] for t in range(n_lt)], axis=1)
                     for k in range(2)], axis=0)
                keys = jnp.concatenate([r3[row], r3[row + 1]], axis=1)
                s = jnp.dot(qb[:, :kv].astype(BF), keys, preferred_element_type=F32) * scale
                sbuf[pl.ds(b * heads, heads), :] = jnp.where(pos < lens[row], s[:heads, :seq], -jnp.inf)
                sbuf[pl.ds((b + 1) * heads, heads), :] = jnp.where(pos < lens[row + 1], s[heads:, seq:], -jnp.inf)
            s = sbuf[...]
            e = jnp.exp(s - jnp.max(s, axis=-1, keepdims=True))
            p = e / jnp.sum(e, axis=-1, keepdims=True)
            pbuf[:, :seq] = jnp.where(first, p, 0.0).astype(BF)
            pbuf[:, seq:] = jnp.where(first, 0.0, p).astype(BF)
            for b in range(0, GRP, 2):
                row = g * GRP + b
                vals = jnp.concatenate([r3[row, 0:latent, :], r3[row + 1, 0:latent, :]], axis=1)
                o = lax.dot_general(pbuf[pl.ds(b * heads, 2 * heads), :], vals, (((1,), (1,)), ((), ())),
                                    preferred_element_type=F32)
                for t in range(latent // 128):
                    o3[t, pl.ds(b, heads, stride=GRP), :] = o[:heads, t * 128:(t + 1) * 128]
                    o3[t, pl.ds(b + 1, heads, stride=GRP), :] = o[heads:, t * 128:(t + 1) * 128]
            for t in range(latent // 128):
                oall[:, pl.ds(pl.multiple_of(g * GRP, GRP), GRP), t * 128:(t + 1) * 128] = (
                    o3[t].astype(BF).reshape(heads, GRP, 128))
            o_copy(g).start()
            return carry

        lax.fori_loop(0, n_grp, attn_group, 0)
        for g in range(n_grp):
            o_copy(g).wait()

        @pl.when(l + 1 < layers)
        def _():
            for g in range(n_grp):
                c_copy(l + 1, g).start()

        def out_block(nb, carry):
            wo_copy(l, nb).wait()
            cols = pl.ds(pl.multiple_of(nb * OBLK, OBLK), OBLK)
            acc = jnp.dot(oall[0], r2[nb, 0:latent, :], preferred_element_type=F32)
            for h in range(1, heads):
                acc = acc + jnp.dot(oall[h], r2[nb, h * latent:(h + 1) * latent, :], preferred_element_type=F32)
            xn = (xfull[c, :, cols].astype(F32) + acc).astype(BF)
            xg[chip, c, pl.ds(pl.multiple_of(c * rows, rows), rows), cols] = xn[:rows]
            xg[chip, c, pl.ds(pl.multiple_of((1 - c) * rows, rows), rows), cols] = xn[rows:]
            return carry

        lax.fori_loop(0, n_ob, out_block, 0)

        pa, pb = pl.ds(0, rows), pl.ds(rows, rows)

        def ag(k, ch, part, dev):
            ref = xg.at[ch, c] if part is None else xg.at[ch, c, part]
            return rc(ref, ref, ag_s.at[k], ag_r.at[k], dev)

        def ag_in(k, ch, half_ix, part):
            ref = xg.at[ch, half_ix] if part is None else xg.at[ch, half_ix, part]
            return rc(ref, ref, ag_s.at[k], ag_r.at[k], partner)

        sends = [ag(0, chip, None, partner), ag(1, chip, pa, right), ag(3, chip, pb, left),
                 ag(2, chip, pb, right), ag(4, chip, pa, left)]
        fwd = [ag(5, ch_l, pa, right), ag(6, ch_r, pb, left), ag(7, ch_l, None, partner),
               ag(8, ch_r, None, partner), ag(9, ch_o, None, partner)]
        for cp in sends:
            cp.start()

        @pl.when(l + 1 < layers)
        def _():
            for nb in range(n_ob):
                wo_copy(l + 1, nb).start()

        ra, rbb = pl.ds(0, rows), pl.ds(rows, rows)
        rs_copies = [
            rc(sown.at[1, rbb], rb.at[0], rs_s.at[0], rs_r.at[0], right),
            rc(sown.at[2, ra], rb.at[1], rs_s.at[1], rs_r.at[1], left),
            rc(sown.at[3, ra], rb.at[2], rs_s.at[2], rs_r.at[2], right),
            rc(sown.at[3, rbb], rb.at[3], rs_s.at[3], rs_r.at[3], left),
            rc(sown.at[1, ra], rb.at[4], rs_s.at[4], rs_r.at[4], right),
            rc(sown.at[2, rbb], rb.at[5], rs_s.at[5], rs_r.at[5], left),
        ]

        def pd_copy(k):
            return rc(pst.at[lax.rem(k, 2)], prd.at[k], pd_s.at[k], pd_r.at[k], partner)

        def pair_sum(k):
            pd_copy(k).wait_recv()
            sown[k] = sown[k] + prd[k]

        for cp in ffn_copies(l):
            cp.wait()

        def chunk(k, carry):
            j = lax.rem(chip + k * (k + 1) // 2, chips)

            @pl.when(k == 0)
            def _():
                ag_in(0, chip, 1 - c, None).wait_recv()

            @pl.when(k == 1)
            def _():
                ag_in(1, ch_l, c, pa).wait_recv()
                fwd[0].start()
                ag_in(3, ch_r, c, pb).wait_recv()
                fwd[1].start()
                ag_in(4, ch_r, c, pa).wait_recv()
                fwd[3].start()
                ag_in(2, ch_l, c, pb).wait_recv()
                fwd[2].start()
                ag_in(8, ch_r, 1 - c, None).wait_recv()

            @pl.when(k == 2)
            def _():
                ag_in(7, ch_l, 1 - c, None).wait_recv()

            @pl.when(k == 3)
            def _():
                ag_in(9, ch_o, 1 - c, None).wait_recv()

            norm_rows(xg.at[j], gf_ref[pl.ds(l, 1), :])
            for lo in range(0, ff, 512):
                w = min(512, ff - lo)
                gate = jnp.dot(hbuf[...], r1[:, lo:lo + w], preferred_element_type=F32)
                up = jnp.dot(hbuf[...], r1[:, ff + lo:ff + lo + w], preferred_element_type=F32)
                hid[:, lo:lo + w] = (jax.nn.silu(gate) * up).astype(BF)

            @pl.when(k == 1)
            def _():
                pair_sum(0)

            @pl.when(k == 2)
            def _():
                pair_sum(1)
                rs_copies[0].start()
                ag_in(5, ch_o, c, pa).wait_recv()
                ag_in(6, ch_o, c, pb).wait_recv()
                fwd[4].start()

            @pl.when(k == 3)
            def _():
                pair_sum(2)
                rs_copies[1].start()

            @pl.when(k >= 2)
            def _():
                pd_copy(k - 2).wait_send()

            slot = lax.rem(k, 2)
            for lo in range(0, half, 512):
                pst[slot, :, lo:lo + 512] = jnp.dot(
                    hid[...], r1[0:ff, 2 * ff + lo:2 * ff + lo + 512], preferred_element_type=F32)
            pd_copy(k).start()
            for lo in range(0, half, 512):
                sown[k, :, lo:lo + 512] = jnp.dot(
                    hid[...], r1[0:ff, 2 * ff + half + lo:2 * ff + half + lo + 512], preferred_element_type=F32)
            return carry

        lax.fori_loop(0, chips, chunk, 0)

        @pl.when(l + 1 < layers)
        def _():
            for i in range(4):
                wq_copy(l + 1, i).start()

        for cp in sends + fwd:
            cp.wait_send()
        pair_sum(3)
        rs_copies[2].start()
        rs_copies[3].start()
        rs_copies[2].wait_recv()
        sown[1, ra] = sown[1, ra] + rb[2]
        rs_copies[4].start()
        rs_copies[3].wait_recv()
        sown[2, rbb] = sown[2, rbb] + rb[3]
        rs_copies[5].start()
        pd_copy(2).wait_send()
        pd_copy(3).wait_send()
        rs_copies[0].wait_recv()
        rs_copies[1].wait_recv()
        sown[0, ra] = sown[0, ra] + rb[1]
        sown[0, rbb] = sown[0, rbb] + rb[0]
        rs_copies[4].wait_recv()
        rs_copies[5].wait_recv()
        mine = pl.ds(pl.multiple_of(c * rows, rows), rows)
        other = pl.ds(pl.multiple_of((1 - c) * rows, rows), rows)
        rb[4] = sown[0, ra] + rb[4] + xg[chip, c, ra].astype(F32)
        rb[5] = sown[0, rbb] + rb[5] + xg[chip, c, rbb].astype(F32)
        xfull[c, pl.ds(0, rows)] = rb[4 + c].astype(BF)
        xfull[c, pl.ds(rows, rows)] = rb[5 - c].astype(BF)
        xx = [rc(xfull.at[c, pl.ds(rows, rows)], xfull.at[c, pl.ds(0, rows)], xx_s.at[0], xx_r.at[0], partner),
              rc(xfull.at[c, pl.ds(0, rows)], xfull.at[c, pl.ds(rows, rows)], xx_s.at[1], xx_r.at[1], partner)]
        for cp in xx:
            cp.start()
        for cp in rs_copies:
            cp.wait_send()
        for cp in xx:
            cp.wait()
        return carry

    lax.fori_loop(0, layers, layer_body, 0)
    x_fin = [pltpu.make_async_copy(xfull.at[k, pl.ds(0, rows)], out_hbm.at[:, pl.ds(k * half, half)], sem_x.at[k])
             for k in range(2)]
    for cp in x_fin:
        cp.start()
    for cp in x_fin:
        cp.wait()


def solution(mesh):
    row_axes = ('replica', 'dp')
    n = mesh.shape['dp']
    chips = n // 2

    def local_step(x_rows, len_rows, cache, attn_gain, ffn_gain, w_query, w_attn_out, w_up, w_gate, w_down):
        layers, rows, seq, kv = cache.shape
        d = x_rows.shape[1]
        heads = w_query.shape[2] // kv
        latent = w_attn_out.shape[1] // heads
        ff = w_up.shape[2]
        half = d // 2
        qh = heads * kv // 2
        dims = (layers, rows, seq, kv, heads, latent, d, ff, chips)
        n_grp = rows // GRP
        n_ob = half // OBLK
        n_lt = pl.cdiv(kv, 128)
        any_spec = pl.BlockSpec(memory_space=pl.ANY)
        vmem = pl.BlockSpec(memory_space=pltpu.VMEM)
        dma = pltpu.SemaphoreType.DMA
        return pl.pallas_call(
            functools.partial(kernel, dims),
            out_shape=jax.ShapeDtypeStruct(x_rows.shape, x_rows.dtype),
            in_specs=[any_spec, pl.BlockSpec(memory_space=pltpu.SMEM), any_spec, vmem, vmem] + [any_spec] * 5,
            out_specs=any_spec,
            scratch_shapes=[
                pltpu.VMEM((d, max(qh, 2 * ff + d)), BF),
                pltpu.VMEM((n_ob, heads * latent, OBLK), BF),
                pltpu.VMEM((rows, kv, seq), BF),
                pltpu.VMEM((2, 2 * rows, half), BF),
                pltpu.VMEM((2 * rows, d), BF),
                pltpu.VMEM((n_lt, heads * rows, 128), F32),
                pltpu.VMEM((n_lt, heads // 2 * rows, 128), F32),
                pltpu.VMEM((GRP * heads, seq), F32),
                pltpu.VMEM((GRP * heads, 2 * seq), BF),
                pltpu.VMEM((latent // 128, GRP * heads, 128), F32),
                pltpu.VMEM((heads, 2 * rows, latent), BF),
                pltpu.VMEM((chips, 2, 2 * rows, half), BF),
                pltpu.VMEM((chips, 2 * rows, half), F32),
                pltpu.VMEM((chips, 2 * rows, half), F32),
                pltpu.VMEM((2, 2 * rows, half), F32),
                pltpu.VMEM((2 * rows, ff), BF),
                pltpu.VMEM((6, rows, half), F32),
                dma((4,)), dma((n_grp,)), dma((n_ob,)), dma((4,)), dma((2,)),
                dma((2,)), dma((2,)), dma((4,)), dma((4,)), dma((n_grp,)), dma((n_grp,)),
                dma((10,)), dma((10,)), dma((chips,)), dma((chips,)), dma((6,)), dma((6,)),
                dma((2,)), dma((2,)),
            ],
            compiler_params=pltpu.CompilerParams(
                collective_id=0, has_side_effects=True, vmem_limit_bytes=67043328),
        )(x_rows, len_rows, jnp.swapaxes(cache, 2, 3), attn_gain, ffn_gain, w_query, w_attn_out, w_up, w_gate, w_down)

    return jax.shard_map(
        local_step,
        mesh=mesh,
        in_specs=(P(row_axes, None), P(row_axes), P(None, row_axes, None, None), P(), P(), P(), P(),
                  P(None, None, 'dp'), P(None, None, 'dp'), P(None, 'dp', None)),
        out_specs=P(row_axes, None),
        check_vma=False,
    )
```

time: 311 us -> 122 us (0.39)
  matrix products: 125 us -> 0 us
  Pallas kernels: 0 us -> 120 us
  waiting for transfers between devices: 115 us -> 0 us
  local copies, waits for them, and re-layouts: 48.1 us -> 1.67 us
  between operations: 13.3 us -> 0.01 us
  other arithmetic: 6.53 us -> 0 us
    dot_general x12 -> x0, matrix products: 125 us -> none  [the longest x2 29.3 us: local_attention(): jnp.dot(normed, wq_l, preferred_element_type=jnp.float32)]
    pallas_call x0 -> x1, Pallas kernels: none -> 120 us  [local_step(): pl.pallas_call(functools.partial(kernel, dims), out_shape=jax.ShapeDtypeS...]
    reduce_scatter x2 -> x0, waiting for transfers between devices: 64.4 us -> none  [local_step(): lax.psum_scatter(partial_out, 'dp', scatter_dimension=0, tiled=True)]
    all_gather x2 -> x0, waiting for transfers between devices: 50.4 us -> none  [local_step(): gathered = lax.all_gather(normed, 'dp', axis=0, tiled=True)]
    slice x5 -> x0, local copies, waits for them, and re-layouts: 45.8 us -> none  [the longest x1 44.7 us: local_step(): w_attn_out[layer_idx]]
    convert_element_type x3 -> x0, other arithmetic: 3.44 us -> none  [the longest x1 1.8 us: local_step(): x_rows = (x_rows.astype(jnp.float32) + ffn_rows).astype(jnp.bfloat16)]
  transfers between devices with their start and end apart: 4 -> 0, of which waited for: 4 -> 0; matrix products, arithmetic and copies ran while one was open for 0% -> 0% of each run, Pallas kernels for 0% -> 0%
where the time goes in v1:
time: 122 us
  Pallas kernels  120 us (98%)
  local copies, waits for them, and re-layouts  1.67 us (1%)
    pallas_call x1, Pallas kernels, local_step(): pl.pallas_call(functools.partial(kernel, dims), out_shape=jax.ShapeDtypeS...  120 us

profile of v1, /device:TPU:81, one launch (start us, length us, event | category | flops | bytes accessed | tf_op | source)
XLA Modules:
  0.0 122.0 jit_solution(5332994427488633501)
XLA Ops:
  0.0 120.3 %shard_map.100 = bf16[64,2048]{1,0:T(8,128)(2,1)} custom-call(bf16[64,2048]{1,0:T(8,128)(2,1)} %x_hbm.1, s32[64]{0:T(128)} %lens.1, bf16[2,64,576,128]{3,2,1,0:T(8,128)(2,1)} %bitcast.1, f32[2,2048]{1,0:T(2,128)} %ga_ref.1, f32[2,2048]{1,0:T(2,128)} %gf_ref.1, bf16[2,2048,9216]{2,1,0:T(8,128)(2,1)} %wq_hbm.1, bf16[2,8192,2048]{2,1,0:T(8,128)(2,1)} %wo_hbm.1, ...), custom_call_target="tpu_custom_call" | custom-call | tf_op jit(solution)/shard_map/pallas_call | solution.py:372
  120.3 1.7 %copy.12 = bf16[64,2048]{1,0:T(8,128)(2,1)} copy(bf16[64,2048]{1,0:T(8,128)(2,1)} %shard_map.100) | data formatting | bytes 524288

commit v2 on v1

v2 whole, which is shorter than its diff:
```python
import functools

import jax
import jax.numpy as jnp
from jax import lax
from jax.experimental import pallas as pl
from jax.experimental.pallas import tpu as pltpu
from jax.sharding import PartitionSpec as P

NORM_EPS = 1e-6
BF = jnp.bfloat16
F32 = jnp.float32
GRP = 16
OBLK = 256


def kernel(dims, x_hbm, len_hbm, cache_hbm, ga_hbm, gf_hbm, wq_hbm, wo_hbm, wu_hbm, wg_hbm, wd_hbm, out_hbm,
           lens, ga_ref, gf_ref, r1, r2, r3, xfull, hbuf, q3, qs, sbuf, pbuf, o3, oall, xg, sown, prd, pst, hid, rb,
           sem_p, sem_w, sem_c, sem_o, sem_f, sem_x, xi_s, xi_r, q_s, q_r, o_s, o_r, ag_s, ag_r, pd_s, pd_r, rs_s, rs_r,
           xx_s, xx_r):
    layers, rows, seq, kv, heads, latent, d, ff, chips = dims
    half = d // 2
    qh = heads * kv // 2
    qblk = qh // 4
    scale = (3 * (kv - latent)) ** -0.5
    n_grp = rows // GRP
    n_ob = half // OBLK
    n_lt = pl.cdiv(kv, 128)

    me = lax.axis_index('dp')
    c = lax.rem(me, 2)
    chip = me // 2
    partner = me + 1 - 2 * c
    right = lax.rem(chip + 1, chips) * 2 + c
    left = lax.rem(chip + chips - 1, chips) * 2 + c
    ch_r = lax.rem(chip + 1, chips)
    ch_l = lax.rem(chip + chips - 1, chips)
    ch_o = lax.rem(chip + 2, chips)

    def rc(src, dst, ss, rs, dev):
        return pltpu.make_async_remote_copy(src_ref=src, dst_ref=dst, send_sem=ss, recv_sem=rs,
                                            device_id={'dp': dev}, device_id_type=pl.DeviceIdType.MESH)

    def wq_copy(l, i):
        cols = pl.ds(pl.multiple_of(c * qh + i * qblk, 128), qblk)
        return pltpu.make_async_copy(wq_hbm.at[l, :, cols], r1.at[:, pl.ds(i * qblk, qblk)], sem_w.at[i])

    def c_copy(l, g):
        rs = pl.ds(pl.multiple_of(g * GRP, GRP), GRP)
        return pltpu.make_async_copy(cache_hbm.at[l, rs], r3.at[rs], sem_c.at[g])

    def wo_copy(l, nb):
        cols = pl.ds(pl.multiple_of(c * half + nb * OBLK, 128), OBLK)
        return pltpu.make_async_copy(wo_hbm.at[l, :, cols], r2.at[nb], sem_o.at[nb])

    def ffn_copies(l):
        lo = pl.ds(pl.multiple_of((1 - c) * half, 128), half)
        hi = pl.ds(pl.multiple_of(c * half, 128), half)
        return (
            pltpu.make_async_copy(wg_hbm.at[l], r1.at[:, pl.ds(0, ff)], sem_f.at[0]),
            pltpu.make_async_copy(wu_hbm.at[l], r1.at[:, pl.ds(ff, ff)], sem_f.at[1]),
            pltpu.make_async_copy(wd_hbm.at[l, :, lo], r1.at[pl.ds(0, ff), pl.ds(2 * ff, half)], sem_f.at[2]),
            pltpu.make_async_copy(wd_hbm.at[l, :, hi], r1.at[pl.ds(0, ff), pl.ds(2 * ff + half, half)], sem_f.at[3]),
        )

    barrier = pltpu.get_barrier_semaphore()
    for dev in (partner, left, right):
        pl.semaphore_signal(barrier, inc=1, device_id={'dp': dev}, device_id_type=pl.DeviceIdType.MESH)
    x_in = [pltpu.make_async_copy(x_hbm.at[:, pl.ds(k * half, half)], xfull.at[k, pl.ds(0, rows)], sem_x.at[k])
            for k in range(2)]
    x_out = [rc(xfull.at[k, pl.ds(0, rows)], xfull.at[k, pl.ds(rows, rows)], xi_s.at[k], xi_r.at[k], partner)
             for k in range(2)]
    small = [pltpu.make_async_copy(ga_hbm, ga_ref, sem_p.at[0]), pltpu.make_async_copy(gf_hbm, gf_ref, sem_p.at[1]),
             pltpu.make_async_copy(len_hbm, lens, sem_p.at[2])]
    for cp in x_in + small:
        cp.start()
    for i in range(4):
        wq_copy(0, i).start()
    pl.semaphore_wait(barrier, 3)
    for k in range(2):
        x_in[k].wait()
        x_out[k].start()
    for cp in small + x_out:
        cp.wait()

    def norm_rows(piece, gain):
        scales = []
        for r in range(2 * rows // 16):
            a, b = (piece(k, r * 16).astype(F32) for k in range(2))
            ms = jnp.sum(a * a + b * b, axis=-1, keepdims=True) * (1.0 / d)
            scales.append(lax.rsqrt(ms + NORM_EPS))
        for r in range(2 * rows // 16):
            for k in range(2):
                hbuf[pl.ds(r * 16, 16), pl.ds(k * half, half)] = (
                    piece(k, r * 16).astype(F32) * scales[r] * gain[:, k * half:(k + 1) * half]).astype(BF)

    def layer_body(l, carry):
        norm_rows(lambda k, r: xfull[k, pl.ds(r, 16), :], ga_ref[pl.ds(l, 1), :])
        q_sends = []
        for i in range(4):
            wq_copy(l, i).wait()

            @pl.when(l == 0)
            def _():
                if i < 2:
                    c_copy(0, 2 * i).start()
                    c_copy(0, 2 * i + 1).start()
                else:
                    wo_copy(0, 2 * (i - 2)).start()
                    wo_copy(0, 2 * (i - 2) + 1).start()

            acc = jnp.dot(hbuf[...], r1[:, i * qblk:(i + 1) * qblk], preferred_element_type=F32)
            acc = acc.astype(BF).astype(F32)
            rolled = pltpu.roll(acc, kv, 1)
            base = pl.multiple_of((c * (heads // 2) + 2 * i) * rows, rows)
            for t in range(n_lt):
                lanes = slice(t * 128, (t + 1) * 128)
                q3[t, pl.ds(base, rows), :] = acc[:rows, lanes]
                q3[t, pl.ds(base + rows, rows), :] = rolled[:rows, lanes]
                qs[t, pl.ds(2 * i * rows, rows), :] = acc[rows:, lanes]
                qs[t, pl.ds((2 * i + 1) * rows, rows), :] = rolled[rows:, lanes]
            cp = rc(qs.at[:, pl.ds(2 * i * rows, 2 * rows)], q3.at[:, pl.ds(base, 2 * rows)], q_s.at[i], q_r.at[i],
                    partner)
            cp.start()
            q_sends.append(cp)
        for cp in ffn_copies(l):
            cp.start()
        for cp in q_sends:
            cp.wait()

        def o_copy(g):
            src = oall.at[:, pl.ds(pl.multiple_of(g * GRP, GRP), GRP)]
            dst = oall.at[:, pl.ds(pl.multiple_of(rows + g * GRP, GRP), GRP)]
            return rc(src, dst, o_s.at[g], o_r.at[g], partner)

        pos = lax.broadcasted_iota(jnp.int32, (heads, seq), 1)
        first = lax.rem(lax.broadcasted_iota(jnp.int32, (GRP * heads, seq), 0), 2 * heads) < heads

        def scores(g, b):
            row = g * GRP + b
            qb = jnp.concatenate(
                [jnp.concatenate([q3[t, pl.ds(row + k, heads, stride=rows), :] for t in range(n_lt)], axis=1)
                 for k in range(2)], axis=0)
            keys = jnp.concatenate([r3[row], r3[row + 1]], axis=1)
            s = jnp.dot(qb[:, :kv].astype(BF), keys, preferred_element_type=F32) * scale
            sbuf[g % 2, pl.ds(b * heads, heads), :] = jnp.where(pos < lens[row], s[:heads, :seq], -jnp.inf)
            sbuf[g % 2, pl.ds((b + 1) * heads, heads), :] = jnp.where(pos < lens[row + 1], s[heads:, seq:], -jnp.inf)

        def mix(g, b):
            row = g * GRP + b
            vals = jnp.concatenate([r3[row, 0:latent, :], r3[row + 1, 0:latent, :]], axis=1)
            o = lax.dot_general(pbuf[pl.ds(b * heads, 2 * heads), :], vals, (((1,), (1,)), ((), ())),
                                preferred_element_type=F32)
            for t in range(latent // 128):
                o3[t, pl.ds(b, heads, stride=GRP), :] = o[:heads, t * 128:(t + 1) * 128]
                o3[t, pl.ds(b + 1, heads, stride=GRP), :] = o[heads:, t * 128:(t + 1) * 128]

        c_copy(l, 0).wait()
        for b in range(0, GRP, 2):
            scores(0, b)
        for g in range(n_grp):
            if g + 1 < n_grp:
                c_copy(l, g + 1).wait()
            s = sbuf[g % 2]
            e = jnp.exp(s - jnp.max(s, axis=-1, keepdims=True))
            p = e / jnp.sum(e, axis=-1, keepdims=True)
            pbuf[:, :seq] = jnp.where(first, p, 0.0).astype(BF)
            pbuf[:, seq:] = jnp.where(first, 0.0, p).astype(BF)
            for b in range(0, GRP, 2):
                if g + 1 < n_grp:
                    scores(g + 1, b)
                mix(g, b)
            for t in range(latent // 128):
                oall[:, pl.ds(g * GRP, GRP), t * 128:(t + 1) * 128] = o3[t].astype(BF).reshape(heads, GRP, 128)
            o_copy(g).start()
        for g in range(n_grp):
            o_copy(g).wait()

        @pl.when(l + 1 < layers)
        def _():
            for g in range(n_grp):
                c_copy(l + 1, g).start()

        pa, pb = pl.ds(0, rows), pl.ds(rows, rows)
        hc = half // 2

        def ag(k, ch, part, dev, hx=None, cols=None):
            hx = c if hx is None else hx
            ref = xg.at[ch, hx] if part is None else xg.at[ch, hx, part]
            if cols is not None:
                ref = xg.at[ch, hx, part, pl.ds(cols * hc, hc)]
            return rc(ref, ref, ag_s.at[k], ag_r.at[k], dev)

        sends = [ag(0, chip, pa, right, cols=0), ag(1, chip, pb, left, cols=0),
                 ag(2, chip, pa, right, cols=1), ag(3, chip, pb, left, cols=1), ag(4, chip, None, partner),
                 ag(5, chip, pb, right), ag(6, chip, pa, left)]
        fwd = [ag(7, ch_l, pa, right), ag(8, ch_r, pb, left), ag(9, ch_l, pa, partner), ag(10, ch_r, pb, partner),
               ag(11, ch_l, pb, partner), ag(12, ch_r, pa, partner), ag(13, ch_o, pa, partner),
               ag(14, ch_o, pb, partner)]

        def got(k, ch, part, hx=None, cols=None):
            ag(k, ch, part, partner, hx, cols).wait_recv()

        for nb in range(n_ob):
            wo_copy(l, nb).wait()
            cols = pl.ds(nb * OBLK, OBLK)
            acc = jnp.dot(oall[0], r2[nb, 0:latent, :], preferred_element_type=F32)
            for h in range(1, heads):
                acc = acc + jnp.dot(oall[h], r2[nb, h * latent:(h + 1) * latent, :], preferred_element_type=F32)
            xn = (xfull[c, :, cols].astype(F32) + acc).astype(BF)
            xg[chip, c, pl.ds(pl.multiple_of(c * rows, rows), rows), cols] = xn[:rows]
            xg[chip, c, pl.ds(pl.multiple_of((1 - c) * rows, rows), rows), cols] = xn[rows:]
            if nb == n_ob // 2 - 1:
                sends[0].start()
                sends[1].start()
        for cp in sends[2:]:
            cp.start()

        @pl.when(l + 1 < layers)
        def _():
            for nb in range(n_ob):
                wo_copy(l + 1, nb).start()

        hr = rows // 2

        def rs_sub(slot, dst, base, sub, k, dev):
            return rc(sown.at[slot, pl.ds(base + sub * hr, hr)], rb.at[dst, pl.ds(sub * hr, hr)],
                      rs_s.at[k], rs_r.at[k], dev)

        unm = [rc(sown.at[1, pa], rb.at[0], rs_s.at[0], rs_r.at[0], left),
               rc(sown.at[1, pb], rb.at[1], rs_s.at[1], rs_r.at[1], right)]
        rly = [rs_sub(2, 2, 0, 0, 2, right), rs_sub(2, 3, rows, 0, 3, left),
               rs_sub(2, 2, 0, 1, 4, right), rs_sub(2, 3, rows, 1, 5, left)]
        mrg = [rs_sub(3, 4, 0, 0, 6, right), rs_sub(3, 5, rows, 0, 7, left),
               rs_sub(3, 4, 0, 1, 8, right), rs_sub(3, 5, rows, 1, 9, left)]

        def pd_copy(k):
            return rc(pst.at[lax.rem(k, 2)], prd.at[k], pd_s.at[k], pd_r.at[k], partner)

        def pair_sum(k):
            pd_copy(k).wait_recv()
            sown[k] = sown[k] + prd[k]

        for cp in ffn_copies(l):
            cp.wait()

        def chunk(k, carry):
            p0 = lax.rem(chip + chips - k, chips)
            p1 = lax.rem(chip + k, chips)

            @pl.when(k == 0)
            def _():
                got(4, chip, None, 1 - c)

            @pl.when(k == 1)
            def _():
                got(0, ch_l, pa, cols=0)
                got(2, ch_l, pa, cols=1)
                fwd[0].start()
                fwd[2].start()
                got(1, ch_r, pb, cols=0)
                got(3, ch_r, pb, cols=1)
                fwd[1].start()
                fwd[3].start()
                pair_sum(0)
                got(9, ch_l, pa, 1 - c)
                got(10, ch_r, pb, 1 - c)

            @pl.when(k == 2)
            def _():
                pair_sum(1)
                unm[0].start()
                unm[1].start()
                got(7, ch_o, pa)
                fwd[6].start()
                got(8, ch_o, pb)
                fwd[7].start()
                got(13, ch_o, pa, 1 - c)
                got(14, ch_o, pb, 1 - c)

            @pl.when(k == 3)
            def _():
                pair_sum(2)
                for cp in rly:
                    cp.start()
                got(11, ch_l, pb, 1 - c)
                got(12, ch_r, pa, 1 - c)

            norm_rows(lambda h, r: xg[p0 if r < rows else p1, h, pl.ds(r, 16), :], gf_ref[pl.ds(l, 1), :])
            for lo in range(0, ff, 512):
                w = min(512, ff - lo)
                gate = jnp.dot(hbuf[...], r1[:, lo:lo + w], preferred_element_type=F32)
                up = jnp.dot(hbuf[...], r1[:, ff + lo:ff + lo + w], preferred_element_type=F32)
                hid[:, lo:lo + w] = (jax.nn.silu(gate) * up).astype(BF)

            @pl.when(k == 1)
            def _():
                got(5, ch_l, pb)
                fwd[4].start()
                got(6, ch_r, pa)
                fwd[5].start()

            @pl.when(k >= 2)
            def _():
                pd_copy(k - 2).wait_send()

            slot = lax.rem(k, 2)
            for lo in range(0, half, 512):
                pst[slot, :, lo:lo + 512] = jnp.dot(
                    hid[...], r1[0:ff, 2 * ff + lo:2 * ff + lo + 512], preferred_element_type=F32)
            pd_copy(k).start()
            for lo in range(0, half, 512):
                sown[k, :, lo:lo + 512] = jnp.dot(
                    hid[...], r1[0:ff, 2 * ff + half + lo:2 * ff + half + lo + 512], preferred_element_type=F32)
            return carry

        lax.fori_loop(0, chips, chunk, 0)

        @pl.when(l + 1 < layers)
        def _():
            for i in range(4):
                wq_copy(l + 1, i).start()

        for cp in sends + fwd:
            cp.wait_send()
        pair_sum(3)
        for i in range(4):
            sub = pl.ds((i // 2) * hr, hr)
            dst = pl.ds((i % 2) * rows + (i // 2) * hr, hr)
            rly[i].wait_recv()
            sown[3, dst] = sown[3, dst] + rb[2 + i % 2, sub]
            mrg[i].start()
        pd_copy(2).wait_send()
        pd_copy(3).wait_send()
        unm[0].wait_recv()
        unm[1].wait_recv()
        rb[0] = rb[0] + sown[0, pa] + xg[chip, c, pa].astype(F32)
        rb[1] = rb[1] + sown[0, pb] + xg[chip, c, pb].astype(F32)
        for cp in mrg:
            cp.wait_recv()
        xfull[c, pl.ds(0, rows)] = (rb[c] + rb[4 + c]).astype(BF)
        xfull[c, pl.ds(rows, rows)] = (rb[1 - c] + rb[5 - c]).astype(BF)
        xx = [rc(xfull.at[c, pl.ds(rows, rows)], xfull.at[c, pl.ds(0, rows)], xx_s.at[0], xx_r.at[0], partner),
              rc(xfull.at[c, pl.ds(0, rows)], xfull.at[c, pl.ds(rows, rows)], xx_s.at[1], xx_r.at[1], partner)]
        for cp in xx:
            cp.start()
        for cp in unm + rly + mrg:
            cp.wait_send()
        for cp in xx:
            cp.wait()
        return carry

    lax.fori_loop(0, layers, layer_body, 0)
    x_fin = [pltpu.make_async_copy(xfull.at[k, pl.ds(0, rows)], out_hbm.at[:, pl.ds(k * half, half)], sem_x.at[k])
             for k in range(2)]
    for cp in x_fin:
        cp.start()
    for cp in x_fin:
        cp.wait()


def solution(mesh):
    row_axes = ('replica', 'dp')
    n = mesh.shape['dp']
    chips = n // 2

    def local_step(x_rows, len_rows, cache, attn_gain, ffn_gain, w_query, w_attn_out, w_up, w_gate, w_down):
        layers, rows, seq, kv = cache.shape
        d = x_rows.shape[1]
        heads = w_query.shape[2] // kv
        latent = w_attn_out.shape[1] // heads
        ff = w_up.shape[2]
        half = d // 2
        qh = heads * kv // 2
        dims = (layers, rows, seq, kv, heads, latent, d, ff, chips)
        n_grp = rows // GRP
        n_ob = half // OBLK
        n_lt = pl.cdiv(kv, 128)
        any_spec = pl.BlockSpec(memory_space=pl.ANY)
        dma = pltpu.SemaphoreType.DMA
        return pl.pallas_call(
            functools.partial(kernel, dims),
            out_shape=jax.ShapeDtypeStruct(x_rows.shape, x_rows.dtype),
            in_specs=[any_spec] * 10,
            out_specs=any_spec,
            scratch_shapes=[
                pltpu.SMEM((rows,), jnp.int32),
                pltpu.VMEM(attn_gain.shape, F32),
                pltpu.VMEM(ffn_gain.shape, F32),
                pltpu.VMEM((d, max(qh, 2 * ff + d)), BF),
                pltpu.VMEM((n_ob, heads * latent, OBLK), BF),
                pltpu.VMEM((rows, kv, seq), BF),
                pltpu.VMEM((2, 2 * rows, half), BF),
                pltpu.VMEM((2 * rows, d), BF),
                pltpu.VMEM((n_lt, heads * rows, 128), F32),
                pltpu.VMEM((n_lt, heads // 2 * rows, 128), F32),
                pltpu.VMEM((2, GRP * heads, seq), F32),
                pltpu.VMEM((GRP * heads, 2 * seq), BF),
                pltpu.VMEM((latent // 128, GRP * heads, 128), F32),
                pltpu.VMEM((heads, 2 * rows, latent), BF),
                pltpu.VMEM((chips, 2, 2 * rows, half), BF),
                pltpu.VMEM((chips, 2 * rows, half), F32),
                pltpu.VMEM((chips, 2 * rows, half), F32),
                pltpu.VMEM((2, 2 * rows, half), F32),
                pltpu.VMEM((2 * rows, ff), BF),
                pltpu.VMEM((6, rows, half), F32),
                dma((3,)), dma((4,)), dma((n_grp,)), dma((n_ob,)), dma((4,)), dma((2,)),
                dma((2,)), dma((2,)), dma((4,)), dma((4,)), dma((n_grp,)), dma((n_grp,)),
                dma((15,)), dma((15,)), dma((chips,)), dma((chips,)), dma((10,)), dma((10,)),
                dma((2,)), dma((2,)),
            ],
            compiler_params=pltpu.CompilerParams(
                collective_id=0, has_side_effects=True, vmem_limit_bytes=67043328),
        )(x_rows, len_rows, jnp.swapaxes(cache, 2, 3), attn_gain, ffn_gain, w_query, w_attn_out, w_up, w_gate, w_down)

    return jax.shard_map(
        local_step,
        mesh=mesh,
        in_specs=(P(row_axes, None), P(row_axes), P(None, row_axes, None, None), P(), P(), P(), P(),
                  P(None, None, 'dp'), P(None, None, 'dp'), P(None, 'dp', None)),
        out_specs=P(row_axes, None),
        check_vma=False,
    )
```

time: 122 us -> 108 us (0.89)
  Pallas kernels: 120 us -> 106 us
    pallas_call x1, Pallas kernels: 120 us -> 106 us  [local_step(): pl.pallas_call(functools.partial(kernel, dims), out_shape=jax.ShapeDtypeS...]
where the time goes in v2:
time: 108 us
  Pallas kernels  106 us (98%)
  local copies, waits for them, and re-layouts  1.67 us (2%)
    pallas_call x1, Pallas kernels, local_step(): pl.pallas_call(functools.partial(kernel, dims), out_shape=jax.ShapeDtypeS...  106 us

profile of v2, /device:TPU:81, one launch (start us, length us, event | category | flops | bytes accessed | tf_op | source)
XLA Modules:
  0.0 107.8 jit_solution(15631381397646955048)
XLA Ops:
  0.0 106.1 %shard_map.100 = bf16[64,2048]{1,0:T(8,128)(2,1)} custom-call(bf16[64,2048]{1,0:T(8,128)(2,1)} %x_hbm.1, s32[64]{0:T(128)} %len_hbm.1, bf16[2,64,576,128]{3,2,1,0:T(8,128)(2,1)} %bitcast.1, f32[2,2048]{1,0:T(2,128)} %ga_hbm.1, f32[2,2048]{1,0:T(2,128)} %gf_hbm.1, bf16[2,2048,9216]{2,1,0:T(8,128)(2,1)} %wq_hbm.1, bf16[2,8192,2048]{2,1,0:T(8,128)(2,1)} %wo_hbm.1, ...), custom_call_target="tpu_custom_call" | custom-call | tf_op jit(solution)/shard_map/pallas_call | solution.py:381
  106.1 1.7 %copy.12 = bf16[64,2048]{1,0:T(8,128)(2,1)} copy(bf16[64,2048]{1,0:T(8,128)(2,1)} %shard_map.100) | data formatting | bytes 524288

commit v3 on v2

--- a/solution.py
+++ b/solution.py
@@ -16,12 +16,12 @@
 
 def kernel(dims, x_hbm, len_hbm, cache_hbm, ga_hbm, gf_hbm, wq_hbm, wo_hbm, wu_hbm, wg_hbm, wd_hbm, out_hbm,
            lens, ga_ref, gf_ref, r1, r2, r3, xfull, hbuf, q3, qs, sbuf, pbuf, o3, oall, xg, sown, prd, pst, hid, rb,
-           sem_p, sem_w, sem_c, sem_o, sem_f, sem_x, xi_s, xi_r, q_s, q_r, o_s, o_r, ag_s, ag_r, pd_s, pd_r, rs_s, rs_r,
+           sem_p, sem_w, sem_c, sem_o, sem_f, sem_x, xi_s, xi_r, q_s, q_r, o_s, o_r, af_s, af_r, ag_s, ag_r, pd_s, pd_r, rs_s, rs_r,
            xx_s, xx_r):
     layers, rows, seq, kv, heads, latent, d, ff, chips = dims
     half = d // 2
     qh = heads * kv // 2
-    qblk = qh // 4
+    qsplit = ((0, heads // 4), (heads // 4, heads // 8), (3 * heads // 8, heads // 8))
     scale = (3 * (kv - latent)) ** -0.5
     n_grp = rows // GRP
     n_ob = half // OBLK
@@ -42,8 +42,9 @@
                                             device_id={'dp': dev}, device_id_type=pl.DeviceIdType.MESH)
 
     def wq_copy(l, i):
-        cols = pl.ds(pl.multiple_of(c * qh + i * qblk, 128), qblk)
-        return pltpu.make_async_copy(wq_hbm.at[l, :, cols], r1.at[:, pl.ds(i * qblk, qblk)], sem_w.at[i])
+        lo, w = qsplit[i][0] * kv, qsplit[i][1] * kv
+        cols = pl.ds(pl.multiple_of(c * qh + lo, 128), w)
+        return pltpu.make_async_copy(wq_hbm.at[l, :, cols], r1.at[:, pl.ds(lo, w)], sem_w.at[i])
 
     def c_copy(l, g):
         rs = pl.ds(pl.multiple_of(g * GRP, GRP), GRP)
@@ -74,12 +75,13 @@
              pltpu.make_async_copy(len_hbm, lens, sem_p.at[2])]
     for cp in x_in + small:
         cp.start()
-    for i in range(4):
+    for cp in x_in:
+        cp.wait()
+    for i in range(3):
         wq_copy(0, i).start()
     pl.semaphore_wait(barrier, 3)
-    for k in range(2):
-        x_in[k].wait()
-        x_out[k].start()
+    for cp in x_out:
+        cp.start()
     for cp in small + x_out:
         cp.wait()
 
@@ -97,29 +99,31 @@
     def layer_body(l, carry):
         norm_rows(lambda k, r: xfull[k, pl.ds(r, 16), :], ga_ref[pl.ds(l, 1), :])
         q_sends = []
-        for i in range(4):
+        for i, (h0, nh) in enumerate(qsplit):
             wq_copy(l, i).wait()
 
             @pl.when(l == 0)
             def _():
-                if i < 2:
-                    c_copy(0, 2 * i).start()
-                    c_copy(0, 2 * i + 1).start()
+                if i == 0:
+                    for g in range(n_grp):
+                        c_copy(0, g).start()
                 else:
-                    wo_copy(0, 2 * (i - 2)).start()
-                    wo_copy(0, 2 * (i - 2) + 1).start()
-
-            acc = jnp.dot(hbuf[...], r1[:, i * qblk:(i + 1) * qblk], preferred_element_type=F32)
+                    for nb in range((i - 1) * n_ob // 2, i * n_ob // 2):
+                        wo_copy(0, nb).start()
+
+            acc = jnp.dot(hbuf[...], r1[:, h0 * kv:(h0 + nh) * kv], preferred_element_type=F32)
             acc = acc.astype(BF).astype(F32)
-            rolled = pltpu.roll(acc, kv, 1)
-            base = pl.multiple_of((c * (heads // 2) + 2 * i) * rows, rows)
-            for t in range(n_lt):
-                lanes = slice(t * 128, (t + 1) * 128)
-                q3[t, pl.ds(base, rows), :] = acc[:rows, lanes]
-                q3[t, pl.ds(base + rows, rows), :] = rolled[:rows, lanes]
-                qs[t, pl.ds(2 * i * rows, rows), :] = acc[rows:, lanes]
-                qs[t, pl.ds((2 * i + 1) * rows, rows), :] = rolled[rows:, lanes]
-            cp = rc(qs.at[:, pl.ds(2 * i * rows, 2 * rows)], q3.at[:, pl.ds(base, 2 * rows)], q_s.at[i], q_r.at[i],
+            base = pl.multiple_of((c * (heads // 2) + h0) * rows, rows)
+            for hh in range(0, nh, 2):
+                two = acc[:, hh * kv:(hh + 2) * kv]
+                rolled = pltpu.roll(two, kv, 1)
+                for t in range(n_lt):
+                    lanes = slice(t * 128, (t + 1) * 128)
+                    q3[t, pl.ds(base + hh * rows, rows), :] = two[:rows, lanes]
+                    q3[t, pl.ds(base + (hh + 1) * rows, rows), :] = rolled[:rows, lanes]
+                    qs[t, pl.ds((h0 + hh) * rows, rows), :] = two[rows:, lanes]
+                    qs[t, pl.ds((h0 + hh + 1) * rows, rows), :] = rolled[rows:, lanes]
+            cp = rc(qs.at[:, pl.ds(h0 * rows, nh * rows)], q3.at[:, pl.ds(base, nh * rows)], q_s.at[i], q_r.at[i],
                     partner)
             cp.start()
             q_sends.append(cp)
@@ -182,38 +186,40 @@
                 c_copy(l + 1, g).start()
 
         pa, pb = pl.ds(0, rows), pl.ds(rows, rows)
-        hc = half // 2
-
-        def ag(k, ch, part, dev, hx=None, cols=None):
+
+        def ag(k, ch, part, dev, hx=None):
             hx = c if hx is None else hx
             ref = xg.at[ch, hx] if part is None else xg.at[ch, hx, part]
-            if cols is not None:
-                ref = xg.at[ch, hx, part, pl.ds(cols * hc, hc)]
             return rc(ref, ref, ag_s.at[k], ag_r.at[k], dev)
 
-        sends = [ag(0, chip, pa, right, cols=0), ag(1, chip, pb, left, cols=0),
-                 ag(2, chip, pa, right, cols=1), ag(3, chip, pb, left, cols=1), ag(4, chip, None, partner),
-                 ag(5, chip, pb, right), ag(6, chip, pa, left)]
+        def ag_first(nb, ch, part, dev):
+            ref = xg.at[ch, c, part, pl.ds(pl.multiple_of(nb * OBLK, OBLK), OBLK)]
+            k = nb if part is pa else n_ob + nb
+            return rc(ref, ref, af_s.at[k], af_r.at[k], dev)
+
+        sends = [ag(4, chip, None, partner), ag(5, chip, pb, right), ag(6, chip, pa, left)]
         fwd = [ag(7, ch_l, pa, right), ag(8, ch_r, pb, left), ag(9, ch_l, pa, partner), ag(10, ch_r, pb, partner),
                ag(11, ch_l, pb, partner), ag(12, ch_r, pa, partner), ag(13, ch_o, pa, partner),
                ag(14, ch_o, pb, partner)]
 
-        def got(k, ch, part, hx=None, cols=None):
-            ag(k, ch, part, partner, hx, cols).wait_recv()
-
-        for nb in range(n_ob):
+        def got(k, ch, part, hx=None):
+            ag(k, ch, part, partner, hx).wait_recv()
+
+        def out_block(nb, carry):
             wo_copy(l, nb).wait()
-            cols = pl.ds(nb * OBLK, OBLK)
+            cols = pl.ds(pl.multiple_of(nb * OBLK, OBLK), OBLK)
             acc = jnp.dot(oall[0], r2[nb, 0:latent, :], preferred_element_type=F32)
             for h in range(1, heads):
                 acc = acc + jnp.dot(oall[h], r2[nb, h * latent:(h + 1) * latent, :], preferred_element_type=F32)
             xn = (xfull[c, :, cols].astype(F32) + acc).astype(BF)
             xg[chip, c, pl.ds(pl.multiple_of(c * rows, rows), rows), cols] = xn[:rows]
             xg[chip, c, pl.ds(pl.multiple_of((1 - c) * rows, rows), rows), cols] = xn[rows:]
-            if nb == n_ob // 2 - 1:
-                sends[0].start()
-                sends[1].start()
-        for cp in sends[2:]:
+            ag_first(nb, chip, pa, right).start()
+            ag_first(nb, chip, pb, left).start()
+            return carry
+
+        lax.fori_loop(0, n_ob, out_block, 0)
+        for cp in (sends[1], sends[2], sends[0]):
             cp.start()
 
         @pl.when(l + 1 < layers)
@@ -227,48 +233,48 @@
             return rc(sown.at[slot, pl.ds(base + sub * hr, hr)], rb.at[dst, pl.ds(sub * hr, hr)],
                       rs_s.at[k], rs_r.at[k], dev)
 
-        unm = [rc(sown.at[1, pa], rb.at[0], rs_s.at[0], rs_r.at[0], left),
-               rc(sown.at[1, pb], rb.at[1], rs_s.at[1], rs_r.at[1], right)]
-        rly = [rs_sub(2, 2, 0, 0, 2, right), rs_sub(2, 3, rows, 0, 3, left),
-               rs_sub(2, 2, 0, 1, 4, right), rs_sub(2, 3, rows, 1, 5, left)]
-        mrg = [rs_sub(3, 4, 0, 0, 6, right), rs_sub(3, 5, rows, 0, 7, left),
-               rs_sub(3, 4, 0, 1, 8, right), rs_sub(3, 5, rows, 1, 9, left)]
-
-        def pd_copy(k):
-            return rc(pst.at[lax.rem(k, 2)], prd.at[k], pd_s.at[k], pd_r.at[k], partner)
-
-        def pair_sum(k):
-            pd_copy(k).wait_recv()
-            sown[k] = sown[k] + prd[k]
+        unm = [rc(sown.at[0, pa], rb.at[0], rs_s.at[0], rs_r.at[0], left),
+               rc(sown.at[0, pb], rb.at[1], rs_s.at[1], rs_r.at[1], right)]
+        rly = [rs_sub(1, 2, 0, 0, 2, right), rs_sub(1, 3, rows, 0, 3, left),
+               rs_sub(1, 2, 0, 1, 4, right), rs_sub(1, 3, rows, 1, 5, left)]
+        mrg = [rs_sub(2, 4, 0, 0, 6, right), rs_sub(2, 5, rows, 0, 7, left),
+               rs_sub(2, 4, 0, 1, 8, right), rs_sub(2, 5, rows, 1, 9, left)]
+
+        hc = half // 2
+
+        def pd_copy(i, hf):
+            cols = pl.ds(hf * hc, hc)
+            return rc(pst.at[lax.rem(i, 2), :, cols], prd.at[i, :, cols], pd_s.at[2 * i + hf], pd_r.at[2 * i + hf],
+                      partner)
+
+        def pair_sum(i):
+            for hf in range(2):
+                pd_copy(i, hf).wait_recv()
+            sown[i] = sown[i] + prd[i]
 
         for cp in ffn_copies(l):
             cp.wait()
 
-        def chunk(k, carry):
-            p0 = lax.rem(chip + chips - k, chips)
-            p1 = lax.rem(chip + k, chips)
-
-            @pl.when(k == 0)
-            def _():
-                got(4, chip, None, 1 - c)
-
-            @pl.when(k == 1)
-            def _():
-                got(0, ch_l, pa, cols=0)
-                got(2, ch_l, pa, cols=1)
+        def chunk(i, carry):
+            p0 = lax.rem(chip + chips - 1 - i, chips)
+            p1 = lax.rem(chip + 1 + i, chips)
+
+            @pl.when(i == 0)
+            def _():
+                for nb in range(n_ob):
+                    ag_first(nb, ch_l, pa, right).wait_recv()
                 fwd[0].start()
                 fwd[2].start()
-                got(1, ch_r, pb, cols=0)
-                got(3, ch_r, pb, cols=1)
+                for nb in range(n_ob):
+                    ag_first(nb, ch_r, pb, left).wait_recv()
                 fwd[1].start()
                 fwd[3].start()
-                pair_sum(0)
                 got(9, ch_l, pa, 1 - c)
                 got(10, ch_r, pb, 1 - c)
 
-            @pl.when(k == 2)
-            def _():
-                pair_sum(1)
+            @pl.when(i == 1)
+            def _():
+                pair_sum(0)
                 unm[0].start()
                 unm[1].start()
                 got(7, ch_o, pa)
@@ -278,13 +284,17 @@
                 got(13, ch_o, pa, 1 - c)
                 got(14, ch_o, pb, 1 - c)
 
-            @pl.when(k == 3)
-            def _():
-                pair_sum(2)
+            @pl.when(i == 2)
+            def _():
+                pair_sum(1)
                 for cp in rly:
                     cp.start()
                 got(11, ch_l, pb, 1 - c)
                 got(12, ch_r, pa, 1 - c)
+
+            @pl.when(i == 3)
+            def _():
+                got(4, chip, None, 1 - c)
 
             norm_rows(lambda h, r: xg[p0 if r < rows else p1, h, pl.ds(r, 16), :], gf_ref[pl.ds(l, 1), :])
             for lo in range(0, ff, 512):
@@ -293,49 +303,58 @@
                 up = jnp.dot(hbuf[...], r1[:, ff + lo:ff + lo + w], preferred_element_type=F32)
                 hid[:, lo:lo + w] = (jax.nn.silu(gate) * up).astype(BF)
 
-            @pl.when(k == 1)
+            @pl.when(i == 0)
             def _():
                 got(5, ch_l, pb)
                 fwd[4].start()
                 got(6, ch_r, pa)
                 fwd[5].start()
 
-            @pl.when(k >= 2)
-            def _():
-                pd_copy(k - 2).wait_send()
-
-            slot = lax.rem(k, 2)
-            for lo in range(0, half, 512):
-                pst[slot, :, lo:lo + 512] = jnp.dot(
-                    hid[...], r1[0:ff, 2 * ff + lo:2 * ff + lo + 512], preferred_element_type=F32)
-            pd_copy(k).start()
-            for lo in range(0, half, 512):
-                sown[k, :, lo:lo + 512] = jnp.dot(
-                    hid[...], r1[0:ff, 2 * ff + half + lo:2 * ff + half + lo + 512], preferred_element_type=F32)
+            @pl.when(i == 3)
+            def _():
+                pair_sum(2)
+
+            @pl.when(i >= 2)
+            def _():
+                for hf in range(2):
+                    pd_copy(i - 2, hf).wait_send()
+
+            slot = lax.rem(i, 2)
+            for hf in range(2):
+                pst[slot, :, hf * hc:(hf + 1) * hc] = jnp.dot(
+                    hid[...], r1[0:ff, 2 * ff + hf * hc:2 * ff + (hf + 1) * hc], preferred_element_type=F32)
+                pd_copy(i, hf).start()
+            for hf in range(2):
+                lo = 2 * ff + half + hf * hc
+                sown[i, :, hf * hc:(hf + 1) * hc] = jnp.dot(hid[...], r1[0:ff, lo:lo + hc], preferred_element_type=F32)
             return carry
 
         lax.fori_loop(0, chips, chunk, 0)
 
         @pl.when(l + 1 < layers)
         def _():
-            for i in range(4):
+            for i in range(3):
                 wq_copy(l + 1, i).start()
 
         for cp in sends + fwd:
             cp.wait_send()
-        pair_sum(3)
+        for nb in range(n_ob):
+            ag_first(nb, chip, pa, right).wait_send()
+            ag_first(nb, chip, pb, left).wait_send()
         for i in range(4):
             sub = pl.ds((i // 2) * hr, hr)
             dst = pl.ds((i % 2) * rows + (i // 2) * hr, hr)
             rly[i].wait_recv()
-            sown[3, dst] = sown[3, dst] + rb[2 + i % 2, sub]
+            sown[2, dst] = sown[2, dst] + rb[2 + i % 2, sub]
             mrg[i].start()
-        pd_copy(2).wait_send()
-        pd_copy(3).wait_send()
+        for i in (2, 3):
+            for hf in range(2):
+                pd_copy(i, hf).wait_send()
+        pair_sum(3)
         unm[0].wait_recv()
         unm[1].wait_recv()
-        rb[0] = rb[0] + sown[0, pa] + xg[chip, c, pa].astype(F32)
-        rb[1] = rb[1] + sown[0, pb] + xg[chip, c, pb].astype(F32)
+        rb[0] = rb[0] + sown[3, pa] + xg[chip, c, pa].astype(F32)
+        rb[1] = rb[1] + sown[3, pb] + xg[chip, c, pb].astype(F32)
         for cp in mrg:
             cp.wait_recv()
         xfull[c, pl.ds(0, rows)] = (rb[c] + rb[4 + c]).astype(BF)
@@ -406,7 +425,7 @@
                 pltpu.VMEM((6, rows, half), F32),
                 dma((3,)), dma((4,)), dma((n_grp,)), dma((n_ob,)), dma((4,)), dma((2,)),
                 dma((2,)), dma((2,)), dma((4,)), dma((4,)), dma((n_grp,)), dma((n_grp,)),
-                dma((15,)), dma((15,)), dma((chips,)), dma((chips,)), dma((10,)), dma((10,)),
+                dma((2 * n_ob,)), dma((2 * n_ob,)), dma((15,)), dma((15,)), dma((2 * chips,)), dma((2 * chips,)), dma((10,)), dma((10,)),
                 dma((2,)), dma((2,)),
             ],
             compiler_params=pltpu.CompilerParams(

time: 108 us -> 101 us (0.935)
  Pallas kernels: 106 us -> 98.9 us
    pallas_call x1, Pallas kernels: 106 us -> 98.9 us  [local_step(): pl.pallas_call(functools.partial(kernel, dims), out_shape=jax.ShapeDtypeS...]
where the time goes in v3:
time: 101 us
  Pallas kernels  98.9 us (98%)
  local copies, waits for them, and re-layouts  1.67 us (2%)
    pallas_call x1, Pallas kernels, local_step(): pl.pallas_call(functools.partial(kernel, dims), out_shape=jax.ShapeDtypeS...  98.9 us

profile of v3, /device:TPU:81, one launch (start us, length us, event | category | flops | bytes accessed | tf_op | source)
XLA Modules:
  0.0 100.6 jit_solution(4998935796950961344)
XLA Ops:
  0.0 98.9 %shard_map.100 = bf16[64,2048]{1,0:T(8,128)(2,1)} custom-call(bf16[64,2048]{1,0:T(8,128)(2,1)} %x_hbm.1, s32[64]{0:T(128)} %len_hbm.1, bf16[2,64,576,128]{3,2,1,0:T(8,128)(2,1)} %bitcast.1, f32[2,2048]{1,0:T(2,128)} %ga_hbm.1, f32[2,2048]{1,0:T(2,128)} %gf_hbm.1, bf16[2,2048,9216]{2,1,0:T(8,128)(2,1)} %wq_hbm.1, bf16[2,8192,2048]{2,1,0:T(8,128)(2,1)} %wo_hbm.1, ...), custom_call_target="tpu_custom_call" | custom-call | tf_op jit(solution)/shard_map/pallas_call | solution.py:400
  99.0 1.7 %copy.12 = bf16[64,2048]{1,0:T(8,128)(2,1)} copy(bf16[64,2048]{1,0:T(8,128)(2,1)} %shard_map.100) | data formatting | bytes 524288

commit v4 on v3

--- a/solution.py
+++ b/solution.py
@@ -11,7 +11,7 @@
 BF = jnp.bfloat16
 F32 = jnp.float32
 GRP = 16
-OBLK = 256
+OBLK = 512
 
 
 def kernel(dims, x_hbm, len_hbm, cache_hbm, ga_hbm, gf_hbm, wq_hbm, wo_hbm, wu_hbm, wg_hbm, wd_hbm, out_hbm,
@@ -20,6 +20,7 @@
            xx_s, xx_r):
     layers, rows, seq, kv, heads, latent, d, ff, chips = dims
     half = d // 2
+    hc = half // 2
     qh = heads * kv // 2
     qsplit = ((0, heads // 4), (heads // 4, heads // 8), (3 * heads // 8, heads // 8))
     scale = (3 * (kv - latent)) ** -0.5
@@ -67,10 +68,9 @@
     barrier = pltpu.get_barrier_semaphore()
     for dev in (partner, left, right):
         pl.semaphore_signal(barrier, inc=1, device_id={'dp': dev}, device_id_type=pl.DeviceIdType.MESH)
-    x_in = [pltpu.make_async_copy(x_hbm.at[:, pl.ds(k * half, half)], xfull.at[k, pl.ds(0, rows)], sem_x.at[k])
-            for k in range(2)]
-    x_out = [rc(xfull.at[k, pl.ds(0, rows)], xfull.at[k, pl.ds(rows, rows)], xi_s.at[k], xi_r.at[k], partner)
-             for k in range(2)]
+    x_in = [pltpu.make_async_copy(x_hbm.at[:, pl.ds(k * hc, hc)], xfull.at[k, pl.ds(0, rows)], sem_x.at[k])
+            for k in range(4)]
+    x_out = [rc(xfull.at[:, pl.ds(0, rows)], xfull.at[:, pl.ds(rows, rows)], xi_s.at[0], xi_r.at[0], partner)]
     small = [pltpu.make_async_copy(ga_hbm, ga_ref, sem_p.at[0]), pltpu.make_async_copy(gf_hbm, gf_ref, sem_p.at[1]),
              pltpu.make_async_copy(len_hbm, lens, sem_p.at[2])]
     for cp in x_in + small:
@@ -88,13 +88,13 @@
     def norm_rows(piece, gain):
         scales = []
         for r in range(2 * rows // 16):
-            a, b = (piece(k, r * 16).astype(F32) for k in range(2))
-            ms = jnp.sum(a * a + b * b, axis=-1, keepdims=True) * (1.0 / d)
+            sq = [piece(k, r * 16).astype(F32) for k in range(4)]
+            ms = jnp.sum(sum(a * a for a in sq), axis=-1, keepdims=True) * (1.0 / d)
             scales.append(lax.rsqrt(ms + NORM_EPS))
         for r in range(2 * rows // 16):
-            for k in range(2):
-                hbuf[pl.ds(r * 16, 16), pl.ds(k * half, half)] = (
-                    piece(k, r * 16).astype(F32) * scales[r] * gain[:, k * half:(k + 1) * half]).astype(BF)
+            for k in range(4):
+                hbuf[pl.ds(r * 16, 16), pl.ds(k * hc, hc)] = (
+                    piece(k, r * 16).astype(F32) * scales[r] * gain[:, k * hc:(k + 1) * hc]).astype(BF)
 
     def layer_body(l, carry):
         norm_rows(lambda k, r: xfull[k, pl.ds(r, 16), :], ga_ref[pl.ds(l, 1), :])
@@ -153,30 +153,34 @@
         def mix(g, b):
             row = g * GRP + b
             vals = jnp.concatenate([r3[row, 0:latent, :], r3[row + 1, 0:latent, :]], axis=1)
-            o = lax.dot_general(pbuf[pl.ds(b * heads, 2 * heads), :], vals, (((1,), (1,)), ((), ())),
+            o = lax.dot_general(pbuf[g % 2, pl.ds(b * heads, 2 * heads), :], vals, (((1,), (1,)), ((), ())),
                                 preferred_element_type=F32)
             for t in range(latent // 128):
                 o3[t, pl.ds(b, heads, stride=GRP), :] = o[:heads, t * 128:(t + 1) * 128]
                 o3[t, pl.ds(b + 1, heads, stride=GRP), :] = o[heads:, t * 128:(t + 1) * 128]
 
-        c_copy(l, 0).wait()
-        for b in range(0, GRP, 2):
-            scores(0, b)
-        for g in range(n_grp):
-            if g + 1 < n_grp:
-                c_copy(l, g + 1).wait()
+        def softmax(g):
             s = sbuf[g % 2]
             e = jnp.exp(s - jnp.max(s, axis=-1, keepdims=True))
             p = e / jnp.sum(e, axis=-1, keepdims=True)
-            pbuf[:, :seq] = jnp.where(first, p, 0.0).astype(BF)
-            pbuf[:, seq:] = jnp.where(first, 0.0, p).astype(BF)
+            pbuf[g % 2, :, :seq] = jnp.where(first, p, 0.0).astype(BF)
+            pbuf[g % 2, :, seq:] = jnp.where(first, 0.0, p).astype(BF)
+
+        for gs in range(n_grp + 2):
+            gx = gs - 2
+            if gs < n_grp:
+                c_copy(l, gs).wait()
+            if 0 < gs <= n_grp:
+                softmax(gs - 1)
             for b in range(0, GRP, 2):
-                if g + 1 < n_grp:
-                    scores(g + 1, b)
-                mix(g, b)
-            for t in range(latent // 128):
-                oall[:, pl.ds(g * GRP, GRP), t * 128:(t + 1) * 128] = o3[t].astype(BF).reshape(heads, GRP, 128)
-            o_copy(g).start()
+                if gs < n_grp:
+                    scores(gs, b)
+                if gx >= 0:
+                    mix(gx, b)
+            if gx >= 0:
+                for t in range(latent // 128):
+                    oall[:, pl.ds(gx * GRP, GRP), t * 128:(t + 1) * 128] = o3[t].astype(BF).reshape(heads, GRP, 128)
+                o_copy(gx).start()
         for g in range(n_grp):
             o_copy(g).wait()
 
@@ -189,12 +193,13 @@
 
         def ag(k, ch, part, dev, hx=None):
             hx = c if hx is None else hx
-            ref = xg.at[ch, hx] if part is None else xg.at[ch, hx, part]
+            quarters = pl.ds(2 * hx, 2)
+            ref = xg.at[ch, quarters] if part is None else xg.at[ch, quarters, part]
             return rc(ref, ref, ag_s.at[k], ag_r.at[k], dev)
 
-        def ag_first(nb, ch, part, dev):
-            ref = xg.at[ch, c, part, pl.ds(pl.multiple_of(nb * OBLK, OBLK), OBLK)]
-            k = nb if part is pa else n_ob + nb
+        def ag_first(hf, ch, part, dev):
+            ref = xg.at[ch, 2 * c + hf, part]
+            k = hf if part is pa else 2 + hf
             return rc(ref, ref, af_s.at[k], af_r.at[k], dev)
 
         sends = [ag(4, chip, None, partner), ag(5, chip, pb, right), ag(6, chip, pa, left)]
@@ -207,19 +212,24 @@
 
         def out_block(nb, carry):
             wo_copy(l, nb).wait()
-            cols = pl.ds(pl.multiple_of(nb * OBLK, OBLK), OBLK)
+            per = hc // OBLK
+            cols = pl.ds(pl.multiple_of(lax.rem(nb, per) * OBLK, OBLK), OBLK)
             acc = jnp.dot(oall[0], r2[nb, 0:latent, :], preferred_element_type=F32)
             for h in range(1, heads):
                 acc = acc + jnp.dot(oall[h], r2[nb, h * latent:(h + 1) * latent, :], preferred_element_type=F32)
-            xn = (xfull[c, :, cols].astype(F32) + acc).astype(BF)
-            xg[chip, c, pl.ds(pl.multiple_of(c * rows, rows), rows), cols] = xn[:rows]
-            xg[chip, c, pl.ds(pl.multiple_of((1 - c) * rows, rows), rows), cols] = xn[rows:]
-            ag_first(nb, chip, pa, right).start()
-            ag_first(nb, chip, pb, left).start()
+            quarter = 2 * c + nb // per
+            xn = (xfull[quarter, :, cols].astype(F32) + acc).astype(BF)
+            xg[chip, quarter, pl.ds(pl.multiple_of(c * rows, rows), rows), cols] = xn[:rows]
+            xg[chip, quarter, pl.ds(pl.multiple_of((1 - c) * rows, rows), rows), cols] = xn[rows:]
+
+            @pl.when(nb == per - 1)
+            def _():
+                ag_first(0, chip, pa, right).start()
+                ag_first(0, chip, pb, left).start()
             return carry
 
         lax.fori_loop(0, n_ob, out_block, 0)
-        for cp in (sends[1], sends[2], sends[0]):
+        for cp in (ag_first(1, chip, pa, right), ag_first(1, chip, pb, left), sends[0], sends[1], sends[2]):
             cp.start()
 
         @pl.when(l + 1 < layers)
@@ -227,56 +237,58 @@
             for nb in range(n_ob):
                 wo_copy(l + 1, nb).start()
 
-        hr = rows // 2
-
-        def rs_sub(slot, dst, base, sub, k, dev):
-            return rc(sown.at[slot, pl.ds(base + sub * hr, hr)], rb.at[dst, pl.ds(sub * hr, hr)],
-                      rs_s.at[k], rs_r.at[k], dev)
-
-        unm = [rc(sown.at[0, pa], rb.at[0], rs_s.at[0], rs_r.at[0], left),
-               rc(sown.at[0, pb], rb.at[1], rs_s.at[1], rs_r.at[1], right)]
-        rly = [rs_sub(1, 2, 0, 0, 2, right), rs_sub(1, 3, rows, 0, 3, left),
-               rs_sub(1, 2, 0, 1, 4, right), rs_sub(1, 3, rows, 1, 5, left)]
-        mrg = [rs_sub(2, 4, 0, 0, 6, right), rs_sub(2, 5, rows, 0, 7, left),
-               rs_sub(2, 4, 0, 1, 8, right), rs_sub(2, 5, rows, 1, 9, left)]
-
-        hc = half // 2
+        def rs(group, slot, hf, way):
+            part, dev = ((pa, right), (pb, left))[way]
+            if group == 0:
+                dev = (left, right)[way]
+            k = group * 4 + hf * 2 + way
+            return rc(sown.at[slot, hf, part], rb.at[2 * group + way, hf], rs_s.at[k], rs_r.at[k], dev)
+
+        unm = [[rs(0, 1, hf, way) for way in range(2)] for hf in range(2)]
+        rly = [[rs(1, 2, hf, way) for way in range(2)] for hf in range(2)]
+        mrg = [[rs(2, 3, hf, way) for way in range(2)] for hf in range(2)]
 
         def pd_copy(i, hf):
-            cols = pl.ds(hf * hc, hc)
-            return rc(pst.at[lax.rem(i, 2), :, cols], prd.at[i, :, cols], pd_s.at[2 * i + hf], pd_r.at[2 * i + hf],
-                      partner)
-
-        def pair_sum(i):
-            for hf in range(2):
-                pd_copy(i, hf).wait_recv()
-            sown[i] = sown[i] + prd[i]
+            return rc(pst.at[lax.rem(i, 2), hf], prd.at[i, hf], pd_s.at[2 * i + hf], pd_r.at[2 * i + hf], partner)
+
+        def pair_sum(i, hf):
+            pd_copy(i, hf).wait_recv()
+            sown[i, hf] = sown[i, hf] + prd[i, hf]
 
         for cp in ffn_copies(l):
             cp.wait()
 
         def chunk(i, carry):
-            p0 = lax.rem(chip + chips - 1 - i, chips)
-            p1 = lax.rem(chip + 1 + i, chips)
+            p0 = lax.rem(chip + chips - i, chips)
+            p1 = lax.rem(chip + i, chips)
 
             @pl.when(i == 0)
             def _():
-                for nb in range(n_ob):
-                    ag_first(nb, ch_l, pa, right).wait_recv()
+                got(4, chip, None, 1 - c)
+
+            @pl.when(i == 1)
+            def _():
+                for hf in range(2):
+                    ag_first(hf, ch_l, pa, right).wait_recv()
                 fwd[0].start()
                 fwd[2].start()
-                for nb in range(n_ob):
-                    ag_first(nb, ch_r, pb, left).wait_recv()
+                for hf in range(2):
+                    ag_first(hf, ch_r, pb, left).wait_recv()
                 fwd[1].start()
                 fwd[3].start()
                 got(9, ch_l, pa, 1 - c)
                 got(10, ch_r, pb, 1 - c)
 
-            @pl.when(i == 1)
-            def _():
-                pair_sum(0)
-                unm[0].start()
-                unm[1].start()
+            @pl.when(i == 2)
+            def _():
+                for hf in range(2):
+                    pair_sum(1, hf)
+                    for cp in unm[hf]:
+                        cp.start()
+                got(5, ch_l, pb)
+                fwd[4].start()
+                got(6, ch_r, pa)
+                fwd[5].start()
                 got(7, ch_o, pa)
                 fwd[6].start()
                 got(8, ch_o, pb)
@@ -284,35 +296,26 @@
                 got(13, ch_o, pa, 1 - c)
                 got(14, ch_o, pb, 1 - c)
 
-            @pl.when(i == 2)
-            def _():
-                pair_sum(1)
-                for cp in rly:
-                    cp.start()
+            @pl.when(i == 3)
+            def _():
+                for hf in range(2):
+                    pair_sum(2, hf)
+                    for cp in rly[hf]:
+                        cp.start()
                 got(11, ch_l, pb, 1 - c)
                 got(12, ch_r, pa, 1 - c)
 
-            @pl.when(i == 3)
-            def _():
-                got(4, chip, None, 1 - c)
-
-            norm_rows(lambda h, r: xg[p0 if r < rows else p1, h, pl.ds(r, 16), :], gf_ref[pl.ds(l, 1), :])
+            norm_rows(lambda q, r: xg[p0 if r < rows else p1, q, pl.ds(r, 16), :], gf_ref[pl.ds(l, 1), :])
             for lo in range(0, ff, 512):
                 w = min(512, ff - lo)
                 gate = jnp.dot(hbuf[...], r1[:, lo:lo + w], preferred_element_type=F32)
                 up = jnp.dot(hbuf[...], r1[:, ff + lo:ff + lo + w], preferred_element_type=F32)
                 hid[:, lo:lo + w] = (jax.nn.silu(gate) * up).astype(BF)
 
-            @pl.when(i == 0)
-            def _():
-                got(5, ch_l, pb)
-                fwd[4].start()
-                got(6, ch_r, pa)
-                fwd[5].start()
-
-            @pl.when(i == 3)
-            def _():
-                pair_sum(2)
+            @pl.when(i == 2)
+            def _():
+                for hf in range(2):
+                    pair_sum(0, hf)
 
             @pl.when(i >= 2)
             def _():
@@ -321,12 +324,12 @@
 
             slot = lax.rem(i, 2)
             for hf in range(2):
-                pst[slot, :, hf * hc:(hf + 1) * hc] = jnp.dot(
+                pst[slot, hf] = jnp.dot(
                     hid[...], r1[0:ff, 2 * ff + hf * hc:2 * ff + (hf + 1) * hc], preferred_element_type=F32)
                 pd_copy(i, hf).start()
             for hf in range(2):
                 lo = 2 * ff + half + hf * hc
-                sown[i, :, hf * hc:(hf + 1) * hc] = jnp.dot(hid[...], r1[0:ff, lo:lo + hc], preferred_element_type=F32)
+                sown[i, hf] = jnp.dot(hid[...], r1[0:ff, lo:lo + hc], preferred_element_type=F32)
             return carry
 
         lax.fori_loop(0, chips, chunk, 0)
@@ -338,40 +341,45 @@
 
         for cp in sends + fwd:
             cp.wait_send()
-        for nb in range(n_ob):
-            ag_first(nb, chip, pa, right).wait_send()
-            ag_first(nb, chip, pb, left).wait_send()
-        for i in range(4):
-            sub = pl.ds((i // 2) * hr, hr)
-            dst = pl.ds((i % 2) * rows + (i // 2) * hr, hr)
-            rly[i].wait_recv()
-            sown[2, dst] = sown[2, dst] + rb[2 + i % 2, sub]
-            mrg[i].start()
+        for hf in range(2):
+            ag_first(hf, chip, pa, right).wait_send()
+            ag_first(hf, chip, pb, left).wait_send()
+        for hf in range(2):
+            pair_sum(3, hf)
+            for way, part in enumerate((pa, pb)):
+                rly[hf][way].wait_recv()
+                sown[3, hf, part] = sown[3, hf, part] + rb[2 + way, hf]
+                mrg[hf][way].start()
         for i in (2, 3):
             for hf in range(2):
                 pd_copy(i, hf).wait_send()
-        pair_sum(3)
-        unm[0].wait_recv()
-        unm[1].wait_recv()
-        rb[0] = rb[0] + sown[3, pa] + xg[chip, c, pa].astype(F32)
-        rb[1] = rb[1] + sown[3, pb] + xg[chip, c, pb].astype(F32)
-        for cp in mrg:
-            cp.wait_recv()
-        xfull[c, pl.ds(0, rows)] = (rb[c] + rb[4 + c]).astype(BF)
-        xfull[c, pl.ds(rows, rows)] = (rb[1 - c] + rb[5 - c]).astype(BF)
-        xx = [rc(xfull.at[c, pl.ds(rows, rows)], xfull.at[c, pl.ds(0, rows)], xx_s.at[0], xx_r.at[0], partner),
-              rc(xfull.at[c, pl.ds(0, rows)], xfull.at[c, pl.ds(rows, rows)], xx_s.at[1], xx_r.at[1], partner)]
-        for cp in xx:
-            cp.start()
-        for cp in unm + rly + mrg:
-            cp.wait_send()
+        for hf in range(2):
+            for way, part in enumerate((pa, pb)):
+                unm[hf][way].wait_recv()
+                rb[way, hf] = rb[way, hf] + sown[0, hf, part] + xg[chip, 2 * c + hf, part].astype(F32)
+        own, oth = pl.ds(0, rows), pl.ds(rows, rows)
+        xx = []
+        for hf in range(2):
+            for way in range(2):
+                mrg[hf][way].wait_recv()
+            ref = xfull.at[2 * c + hf]
+            xfull[2 * c + hf, own] = (rb[c, hf] + rb[4 + c, hf]).astype(BF)
+            xfull[2 * c + hf, oth] = (rb[1 - c, hf] + rb[5 - c, hf]).astype(BF)
+            for k, (a, b) in enumerate(((oth, own), (own, oth))):
+                cp = rc(ref.at[a], ref.at[b], xx_s.at[2 * hf + k], xx_r.at[2 * hf + k], partner)
+                cp.start()
+                xx.append(cp)
+        for group in (unm, rly, mrg):
+            for hf in range(2):
+                for cp in group[hf]:
+                    cp.wait_send()
         for cp in xx:
             cp.wait()
         return carry
 
     lax.fori_loop(0, layers, layer_body, 0)
-    x_fin = [pltpu.make_async_copy(xfull.at[k, pl.ds(0, rows)], out_hbm.at[:, pl.ds(k * half, half)], sem_x.at[k])
-             for k in range(2)]
+    x_fin = [pltpu.make_async_copy(xfull.at[k, pl.ds(0, rows)], out_hbm.at[:, pl.ds(k * hc, hc)], sem_x.at[k])
+             for k in range(4)]
     for cp in x_fin:
         cp.start()
     for cp in x_fin:
@@ -409,24 +417,24 @@
                 pltpu.VMEM((d, max(qh, 2 * ff + d)), BF),
                 pltpu.VMEM((n_ob, heads * latent, OBLK), BF),
                 pltpu.VMEM((rows, kv, seq), BF),
-                pltpu.VMEM((2, 2 * rows, half), BF),
+                pltpu.VMEM((4, 2 * rows, half // 2), BF),
                 pltpu.VMEM((2 * rows, d), BF),
                 pltpu.VMEM((n_lt, heads * rows, 128), F32),
                 pltpu.VMEM((n_lt, heads // 2 * rows, 128), F32),
                 pltpu.VMEM((2, GRP * heads, seq), F32),
-                pltpu.VMEM((GRP * heads, 2 * seq), BF),
+                pltpu.VMEM((2, GRP * heads, 2 * seq), BF),
                 pltpu.VMEM((latent // 128, GRP * heads, 128), F32),
                 pltpu.VMEM((heads, 2 * rows, latent), BF),
-                pltpu.VMEM((chips, 2, 2 * rows, half), BF),
-                pltpu.VMEM((chips, 2 * rows, half), F32),
-                pltpu.VMEM((chips, 2 * rows, half), F32),
-                pltpu.VMEM((2, 2 * rows, half), F32),
+                pltpu.VMEM((chips, 4, 2 * rows, half // 2), BF),
+                pltpu.VMEM((chips, 2, 2 * rows, half // 2), F32),
+                pltpu.VMEM((chips, 2, 2 * rows, half // 2), F32),
+                pltpu.VMEM((2, 2, 2 * rows, half // 2), F32),
                 pltpu.VMEM((2 * rows, ff), BF),
-                pltpu.VMEM((6, rows, half), F32),
-                dma((3,)), dma((4,)), dma((n_grp,)), dma((n_ob,)), dma((4,)), dma((2,)),
+                pltpu.VMEM((6, 2, rows, half // 2), F32),
+                dma((3,)), dma((4,)), dma((n_grp,)), dma((n_ob,)), dma((4,)), dma((4,)),
                 dma((2,)), dma((2,)), dma((4,)), dma((4,)), dma((n_grp,)), dma((n_grp,)),
-                dma((2 * n_ob,)), dma((2 * n_ob,)), dma((15,)), dma((15,)), dma((2 * chips,)), dma((2 * chips,)), dma((10,)), dma((10,)),
-                dma((2,)), dma((2,)),
+                dma((4,)), dma((4,)), dma((15,)), dma((15,)), dma((2 * chips,)), dma((2 * chips,)), dma((12,)), dma((12,)),
+                dma((4,)), dma((4,)),
             ],
             compiler_params=pltpu.CompilerParams(
                 collective_id=0, has_side_effects=True, vmem_limit_bytes=67043328),

time: 101 us -> 99.9 us (0.989)
  no operation moved by 1% of the time
where the time goes in v4:
time: 99.9 us; the launch traced here: 99.8 us
  Pallas kernels  98.1 us (98%)
  local copies, waits for them, and re-layouts  1.67 us (2%)
    pallas_call x1, Pallas kernels, local_step(): pl.pallas_call(functools.partial(kernel, dims), out_shape=jax.ShapeDtypeS...  98.1 us

profile of v4, /device:TPU:81, one launch (start us, length us, event | category | flops | bytes accessed | tf_op | source)
XLA Modules:
  0.0 99.8 jit_solution(12866460565994692343)
XLA Ops:
  0.0 98.1 %shard_map.100 = bf16[64,2048]{1,0:T(8,128)(2,1)} custom-call(bf16[64,2048]{1,0:T(8,128)(2,1)} %x_hbm.1, s32[64]{0:T(128)} %len_hbm.1, bf16[2,64,576,128]{3,2,1,0:T(8,128)(2,1)} %bitcast.1, f32[2,2048]{1,0:T(2,128)} %ga_hbm.1, f32[2,2048]{1,0:T(2,128)} %gf_hbm.1, bf16[2,2048,9216]{2,1,0:T(8,128)(2,1)} %wq_hbm.1, bf16[2,8192,2048]{2,1,0:T(8,128)(2,1)} %wo_hbm.1, ...), custom_call_target="tpu_custom_call" | custom-call | tf_op jit(solution)/shard_map/pallas_call | solution.py:408
  98.1 1.7 %copy.12 = bf16[64,2048]{1,0:T(8,128)(2,1)} copy(bf16[64,2048]{1,0:T(8,128)(2,1)} %shard_map.100) | data formatting | bytes 524288
